TPU v7x, 128 devices: a whole 4x4x4 slice. The times are simulated.
128 devices in a mesh: row: 8 (over z, x_lo), col: 16 (over y, x_hi, core).
Axes of the slice: x: 4 (x_hi: 2, x_lo: 2; x = x_hi * 2 + x_lo), y: 4, z: 4, core: 2. Of those that a mesh axis runs over, the one named last changes fastest.
Arguments:
- cell_index: int32 [2, 3, 262144], P(None, None, ('row', 'col')), may hold values from 0 to 255, as said below
- fraction: float32 [2, 3, 262144], P(None, None, ('row', 'col')), may hold values from 0 to 1
- charge: float32 [2, 262144], P(None, ('row', 'col')), may hold values from -4 to 4
- atom_count: int32 [2, 128], P(None, ('row', 'col')), may hold values from 1024 to 2048, as said below
- influence: float32 [256, 256, 256], P('row', 'col'), as said below
Outputs:
- forces: float32 [2, 3, 262144], P(None, None, ('row', 'col'))
Inputs may be any that keep to these rules, and one draw needn't show every extreme that they name: `cell_index`: slot a belongs to pencil p = a // 2048; with P = 16, its first cell index lies in [(p // P) * 32, (p // P + 1) * 32) and its second in [(p % P) * 16, (p % P + 1) * 16). `atom_count`: in every frame some pencil has all 2048 slots live. Even: influence[a, b, c] equals influence[(-a) mod 256, (-b) mod 256, (-c) mod 256]; it is 0 at the root and positive elsewhere.
All inputs are finite; a program needn't handle non-finite values.
Results may differ from a plain program's by a relative error of at most 0.0003.
Values sent between devices are 32-bit elements; how exact they have to be, the bound alone decides.
No kernel may reach another device: no remote copies, remote signals or barrier semaphores. Data moves between devices by JAX's collectives and lax.ppermute only.
A program may use at most 128 MiB of HBM per device.

v0:
```python
import math

import jax
import jax.numpy as jnp
import numpy as np
from jax import lax
from jax.experimental import pallas as pl
from jax.experimental.pallas import tpu as pltpu
from jax.sharding import PartitionSpec as P

F32 = jnp.float32
BF16 = jnp.bfloat16
K = 256
XB = 32
YB = 16
ROWS = 8
COLS = 16
DEV = ROWS * COLS
ATOMS = 2048
CHUNK = 512
RIM = 5
INNER = XB * YB
XRIM = RIM * YB
YRIM = RIM * XB
CRIM = RIM * 8
RIMS = XRIM + YRIM + CRIM
VMEM_ALL = pl.BlockSpec(memory_space=pltpu.VMEM)
SMEM_ALL = pl.BlockSpec(memory_space=pltpu.SMEM)


def halves(values):
    top = values.astype(np.float32).astype(jnp.bfloat16)
    rest = (values - top.astype(np.float64)).astype(np.float32).astype(jnp.bfloat16)
    return top, rest


def z_tables():
    p, d = np.meshgrid(np.arange(2), np.arange(DEV), indexing="ij")
    kz = (16 * (d % COLS) + 2 * (d // COLS) + p).reshape(-1)
    angle = 2.0 * math.pi * ((kz[:, None] * np.arange(K)[None, :]) % K) / K
    return halves(np.cos(angle)) + halves(np.sin(angle))


def x_tables():
    x = np.arange(K)
    angle = 2.0 * math.pi * ((x[:, None] * x[None, :]) % K) / K
    return halves(np.cos(angle)) + halves(np.sin(angle))


def y_table():
    c, low, part, high = np.meshgrid(
        np.arange(COLS), np.arange(4), np.arange(2), np.arange(4), indexing="ij"
    )
    y = (16 * c + 4 * high + low).reshape(-1)
    part = part.reshape(-1)[None, :]
    angle = 2.0 * math.pi * ((np.arange(K)[:, None] * y[None, :]) % K) / K
    cosine, sine = np.cos(angle), np.sin(angle)
    real = np.where(part == 0, cosine, sine)
    imag = np.where(part == 0, -sine, cosine)
    return np.concatenate([real, imag], axis=0)


def split(value):
    top = value.astype(BF16)
    return top, (value - top.astype(F32)).astype(BF16)


def dot(a, b, dims=((1,), (0,))):
    return lax.dot_general(a, b, (dims, ((), ())), preferred_element_type=F32)


def dot3(a, b, dims=((1,), (0,))):
    return dot(a[0], b[0], dims) + dot(a[0], b[1], dims) + dot(a[1], b[0], dims)


def spline_values(fraction):
    nothing = jnp.zeros_like(fraction)
    levels = [fraction, 1.0 - fraction]
    slopes = levels
    for degree in range(3, 7):
        padded = levels + [nothing]
        following = []
        for offset in range(degree):
            beneath = padded[offset - 1] if offset > 0 else nothing
            following.append(
                ((fraction + offset) * padded[offset] + (degree - fraction - offset) * beneath)
                * (1.0 / (degree - 1))
            )
        if degree == 6:
            slopes = [
                padded[offset] - (padded[offset - 1] if offset > 0 else nothing)
                for offset in range(6)
            ]
        levels = following
    return levels, slopes


def placed_rows(cell, values, first, count, wrapped):
    shape = (count, cell.shape[1])
    behind = cell - (lax.broadcasted_iota(jnp.int32, shape, 0) + first)
    if wrapped:
        behind = behind & (K - 1)
    masks = [behind == j for j in range(6)]
    results = []
    for value in values:
        total = jnp.zeros(shape, F32)
        for j in range(6):
            total = jnp.where(masks[j], value[j], total)
        results.append(total)
    return results


def atom_slice(cell_ref, frac_ref, charge_ref, count_ref, s, at):
    lanes = pl.ds(pl.multiple_of(at, CHUNK), CHUNK)
    cells = cell_ref[s, :, lanes]
    levels, slopes = spline_values(frac_ref[s, :, lanes])
    slots = lax.broadcasted_iota(jnp.int32, (1, CHUNK), 1) + at
    charges = jnp.where(slots < count_ref[s, 0], charge_ref[pl.ds(s, 1), lanes], 0.0)

    def dimension(d):
        return [w[d : d + 1] for w in levels], [w[d : d + 1] for w in slopes]

    return cells, dimension, charges


def spread_kernel(count_ref, cell_ref, frac_ref, charge_ref, mesh_ref, xr_ref, yr_ref, cr_ref, ph, pq):
    s, i = pl.program_id(0), pl.program_id(1)
    cells, dimension, charges = atom_slice(cell_ref, frac_ref, charge_ref, count_ref, s, i * CHUNK)
    (first,) = placed_rows(cells[0:1] & (XB - 1), [dimension(0)[0]], -8, XB + 8, False)
    (second,) = placed_rows(cells[1:2] & (YB - 1), [dimension(1)[0]], -8, YB + 8, False)
    (third,) = placed_rows(cells[2:3], [dimension(2)[0]], 0, K, True)
    third = split(third)
    second = second * charges

    def put(at, product):
        top, rest = split(product)
        ph[at : at + product.shape[0], :] = top
        pq[at : at + product.shape[0], :] = rest

    for y in range(YB):
        put(y * XB, second[8 + y : 9 + y] * first[8:])
    for x in range(RIM):
        put(INNER + x * YB, first[3 + x : 4 + x] * second[8:])
    for y in range(RIM):
        put(INNER + XRIM + y * XB, second[3 + y : 4 + y] * first[8:])
    corner = [second[3 + y : 4 + y] * first[:8] for y in range(RIM)] + [jnp.zeros((8, CHUNK), F32)]
    for y in range(0, RIM + 1, 2):
        put(INNER + XRIM + YRIM + y * 8, jnp.concatenate(corner[y : y + 2], axis=0))

    total = dot3((ph[...], pq[...]), third, ((1,), (1,)))
    pieces = (
        (mesh_ref, 0, INNER),
        (xr_ref, INNER, XRIM),
        (yr_ref, INNER + XRIM, YRIM),
        (cr_ref, INNER + XRIM + YRIM, CRIM),
    )

    @pl.when(i == 0)
    def _():
        for ref, at, count in pieces:
            for h in range(2):
                ref[2 * s + h] = total[at : at + count, h * 128 : h * 128 + 128]

    @pl.when(i > 0)
    def _():
        for ref, at, count in pieces:
            for h in range(2):
                ref[2 * s + h] += total[at : at + count, h * 128 : h * 128 + 128]


def forward_z_kernel(mesh_ref, xr_ref, yr_ref, cr_ref, ch, cl, sh, sl, out_ref, m):
    m[...] = mesh_ref[...]
    parts = []
    for s in range(2):
        base = (YB - RIM) * XB
        columns = []
        for h in range(2):
            k = 2 * s + h
            m[k, base : base + YRIM, :] += yr_ref[k]
            for x in range(RIM):
                rows = pl.ds(XB - RIM + x, YB, stride=XB)
                m[k, rows, :] += xr_ref[k, x * YB : x * YB + YB, :]
            for y in range(RIM):
                at = (YB - RIM + y) * XB + XB - 8
                m[k, at : at + 8, :] += cr_ref[k, y * 8 : y * 8 + 8]
            columns.append(m[k].T)
        parts.append(split(jnp.concatenate(columns, axis=0)))
    cosines, sines = (ch[...], cl[...]), (sh[...], sl[...])
    real = dot3(cosines, parts[0]) + dot3(sines, parts[1])
    imag = dot3(cosines, parts[1]) - dot3(sines, parts[0])
    for q, value in enumerate((real, imag)):
        for p in range(2):
            for b in range(4):
                out_ref[pl.ds(p * 8 + q * 4 + b, DEV, stride=16), :] = value[
                    p * DEV : (p + 1) * DEV, b * 128 : (b + 1) * 128
                ]


def exchange_blocks(pieces):
    lane = lax.broadcasted_iota(jnp.int32, pieces[0].shape, 1)
    for bit in (1, 2):
        upper = (lane // 32) & bit == bit
        fresh = list(pieces)
        for v in range(4):
            if v & bit == 0:
                a, b = pieces[v], pieces[v | bit]
                fresh[v] = jnp.where(upper, pltpu.roll(b, 32 * bit, 1), a)
                fresh[v | bit] = jnp.where(upper, b, pltpu.roll(a, 128 - 32 * bit, 1))
        pieces = fresh
    return pieces


def plane_kernel(buf_ref, green_ref, eh, el, th, tl, ch, cl, sh, sl, out_ref, d, o):
    cosines, sines = (ch[...], cl[...]), (sh[...], sl[...])
    for p in range(2):
        for c in range(COLS):
            for g in range(2):
                tiles = []
                for r in range(4):
                    at = ((g * 4 + r) * COLS + c) * 16 + p * 8
                    tiles.append(buf_ref[at : at + 8, :])
                for low, tile in enumerate(exchange_blocks(tiles)):
                    at = (c * 4 + low) * 8
                    d[at : at + 8, g * 128 : g * 128 + 128] = tile
        first = dot3((eh[...], el[...]), split(d[...]))
        real, imag = split(first[:K]), split(first[K:])
        f_real = dot3(real, cosines) + dot3(imag, sines)
        f_imag = dot3(imag, cosines) - dot3(real, sines)
        green = jnp.concatenate(
            [green_ref[(r * 2 + p) * XB : (r * 2 + p + 1) * XB, :] for r in range(ROWS)], axis=0
        ) * (1.0 / float(K) ** 3)
        real, imag = split(f_real * green), split(f_imag * green)
        t_real = split(dot3(real, cosines) - dot3(imag, sines))
        t_imag = split(dot3(imag, cosines) + dot3(real, sines))
        both = tuple(jnp.concatenate([a, b], axis=0) for a, b in zip(t_real, t_imag))
        o[...] = dot3((th[...], tl[...]), both)
        for c in range(COLS):
            for g in range(2):
                tiles = []
                for low in range(4):
                    at = (c * 4 + low) * 8
                    tiles.append(o[at : at + 8, g * 128 : g * 128 + 128])
                for r, tile in enumerate(exchange_blocks(tiles)):
                    at = ((g * 4 + r) * COLS + c) * 16 + p * 8
                    out_ref[at : at + 8, :] = tile


def inverse_z_kernel(buf_ref, ch, cl, sh, sl, field_ref, xr_ref, yr_ref, cr_ref):
    cosines, sines = (ch[...], cl[...]), (sh[...], sl[...])
    parts = []
    for q in range(2):
        columns = []
        for p in range(2):
            blocks = []
            for b in range(4):
                blocks.append(buf_ref[pl.ds(p * 8 + q * 4 + b, DEV, stride=16), :].T)
            columns.append(jnp.concatenate(blocks, axis=0))
        parts.append(split(jnp.concatenate(columns, axis=1)))
    real, imag = parts
    fields = (
        dot3(real, cosines) - dot3(imag, sines),
        dot3(imag, cosines) + dot3(real, sines),
    )
    base = (YB - RIM) * XB
    for k in range(4):
        field_ref[k] = fields[k // 2][:, k % 2 * 128 : k % 2 * 128 + 128]
        yr_ref[k] = field_ref[k, base : base + YRIM, :]
        for x in range(RIM):
            rows = pl.ds(XB - RIM + x, YB, stride=XB)
            xr_ref[k, x * YB : x * YB + YB, :] = field_ref[k, rows, :]
        for y in range(RIM):
            at = (YB - RIM + y) * XB + XB - 8
            cr_ref[k, y * 8 : y * 8 + 8, :] = field_ref[k, at : at + 8, :]


def gather_kernel(count_ref, cell_ref, frac_ref, charge_ref, field_ref, xr_ref, yr_ref, cr_ref, out_ref, fh, fl):
    s, i = pl.program_id(0), pl.program_id(1)

    @pl.when(i == 0)
    def _():
        pieces = (
            (field_ref, 0, INNER),
            (xr_ref, INNER, XRIM),
            (yr_ref, INNER + XRIM, YRIM),
        )
        for h in range(2):
            lanes = slice(h * 128, h * 128 + 128)
            for ref, at, count in pieces:
                top, rest = split(ref[2 * s + h])
                fh[at : at + count, lanes] = top
                fl[at : at + count, lanes] = rest
            at = INNER + XRIM + YRIM
            values = jnp.concatenate([cr_ref[2 * s + h], jnp.zeros((8, 128), F32)], axis=0)
            top, rest = split(values)
            fh[at : at + CRIM + 8, lanes] = top
            fl[at : at + CRIM + 8, lanes] = rest

    at = i * CHUNK
    cells, dimension, charges = atom_slice(cell_ref, frac_ref, charge_ref, count_ref, s, at)
    w1, s1 = placed_rows(cells[0:1] & (XB - 1), dimension(0), -8, XB + 8, False)
    w2, s2 = placed_rows(cells[1:2] & (YB - 1), dimension(1), -8, YB + 8, False)
    w3, s3 = placed_rows(cells[2:3], dimension(2), 0, K, True)
    field = (fh[...], fl[...])
    plain = dot3(field, split(w3))
    sloped = dot3(field, split(s3))

    def gathered(base, size, along, across):
        sums = [jnp.zeros((size, CHUNK), F32) for _ in range(3)]
        for n, (value, slope) in enumerate(along):
            rows = slice(base + n * size, base + (n + 1) * size)
            sums[0] += value * plain[rows]
            sums[1] += slope * plain[rows]
            sums[2] += value * sloped[rows]
        value, slope = across
        return (
            jnp.sum(sums[0] * slope, axis=0, keepdims=True),
            jnp.sum(sums[1] * value, axis=0, keepdims=True),
            jnp.sum(sums[2] * value, axis=0, keepdims=True),
        )

    def row(pair, n):
        return pair[0][n : n + 1], pair[1][n : n + 1]

    xs, ys = (w1, s1), (w2, s2)
    inner = gathered(0, XB, [row(ys, 8 + y) for y in range(YB)], (w1[8:], s1[8:]))
    side = gathered(INNER, YB, [row(xs, 3 + x) for x in range(RIM)], (w2[8:], s2[8:]))
    edge = gathered(INNER + XRIM, XB, [row(ys, 3 + y) for y in range(RIM)], (w1[8:], s1[8:]))
    corner = gathered(INNER + XRIM + YRIM, 8, [row(ys, 3 + y) for y in range(RIM)], (w1[:8], s1[:8]))
    force_x = inner[0] + side[1] + edge[0] + corner[0]
    force_y = inner[1] + side[0] + edge[1] + corner[1]
    force_z = inner[2] + side[2] + edge[2] + corner[2]
    lanes = pl.ds(pl.multiple_of(at, CHUNK), CHUNK)
    out_ref[s, :, lanes] = -charges * jnp.concatenate([force_x, force_y, force_z], axis=0)


def green_kernel(in_ref, out_ref, m):
    for h in range(2):
        lanes = slice(h * 128, h * 128 + 128)
        m[...] = in_ref[:, lanes]
        for k in range(COLS):
            out_ref[k * XB : (k + 1) * XB, lanes] = m[pl.ds(k, XB, stride=COLS), :]


def cost(flops, size):
    return pl.CostEstimate(flops=int(flops), bytes_accessed=int(size), transcendentals=0)


def shape(*dims):
    return jax.ShapeDtypeStruct(dims, F32)


def params(steps=0):
    if steps:
        return pltpu.CompilerParams(dimension_semantics=("arbitrary",) * steps)
    return pltpu.CompilerParams()


def shift(value, rows, cols):
    pairs = []
    for r in range(ROWS):
        for c in range(COLS):
            pairs.append((r * COLS + c, ((r + rows) % ROWS) * COLS + (c + cols) % COLS))
    return lax.ppermute(value, ("row", "col"), pairs)


def everywhere(value):
    return lax.all_to_all(value, ("row", "col"), split_axis=0, concat_axis=0, tiled=True)


def shards(cell_index, fraction, charge, atom_count, influence):
    zc = [jnp.asarray(t) for t in z_tables()]
    xc = [jnp.asarray(t) for t in x_tables()]
    table = y_table()
    ye = [jnp.asarray(t) for t in halves(table)]
    yt = [jnp.asarray(t) for t in halves(np.ascontiguousarray(table.T))]

    green = pl.pallas_call(
        green_kernel,
        out_shape=shape(512, K),
        in_specs=[VMEM_ALL],
        out_specs=VMEM_ALL,
        scratch_shapes=[pltpu.VMEM((512, 128), F32)],
        compiler_params=params(),
        cost_estimate=cost(1e6, 2**20),
        name="green",
    )(influence.reshape(XB * COLS, K))
    green = lax.all_to_all(
        green.reshape(ROWS, 64, K), "row", split_axis=0, concat_axis=0, tiled=True
    ).reshape(512, K)

    atoms_specs = [SMEM_ALL, VMEM_ALL, VMEM_ALL, VMEM_ALL]
    atoms = (atom_count, cell_index, fraction, charge)
    steps = ATOMS // CHUNK
    rim_shapes = [shape(4, XRIM, 128), shape(4, YRIM, 128), shape(4, CRIM, 128)]
    mesh, xr, yr, cr = pl.pallas_call(
        spread_kernel,
        grid=(2, steps),
        out_shape=[shape(4, INNER, 128)] + rim_shapes,
        in_specs=atoms_specs,
        out_specs=[VMEM_ALL] * 4,
        scratch_shapes=[pltpu.VMEM((INNER + RIMS + 8, CHUNK), BF16)] * 2,
        compiler_params=params(2),
        cost_estimate=cost(1.0e10, 2**21),
        name="spread",
    )(*atoms)
    xr, yr, cr = shift(xr, -1, 0), shift(yr, 0, -1), shift(cr, -1, -1)
    packed = pl.pallas_call(
        forward_z_kernel,
        out_shape=shape(DEV * 16, 128),
        in_specs=[VMEM_ALL] * 8,
        out_specs=VMEM_ALL,
        scratch_shapes=[pltpu.VMEM((4, INNER, 128), F32)],
        compiler_params=params(),
        cost_estimate=cost(2.0e9, 2**22),
        name="forward_z",
    )(mesh, xr, yr, cr, *zc)
    packed = everywhere(packed.reshape(DEV, 16, 128)).reshape(DEV * 16, 128)
    packed = pl.pallas_call(
        plane_kernel,
        out_shape=shape(DEV * 16, 128),
        in_specs=[VMEM_ALL] * 10,
        out_specs=VMEM_ALL,
        scratch_shapes=[pltpu.VMEM((512, K), F32)] * 2,
        compiler_params=params(),
        cost_estimate=cost(4.0e9, 2**23),
        name="planes",
    )(packed, green, *ye, *yt, *xc)
    packed = everywhere(packed.reshape(DEV, 16, 128)).reshape(DEV * 16, 128)
    field, xr, yr, cr = pl.pallas_call(
        inverse_z_kernel,
        out_shape=[shape(4, INNER, 128)] + rim_shapes,
        in_specs=[VMEM_ALL] * 5,
        out_specs=[VMEM_ALL] * 4,
        compiler_params=params(),
        cost_estimate=cost(2.0e9, 2**22),
        name="inverse_z",
    )(packed, *zc)
    xr, yr, cr = shift(xr, 1, 0), shift(yr, 0, 1), shift(cr, 1, 1)
    return pl.pallas_call(
        gather_kernel,
        grid=(2, steps),
        out_shape=shape(2, 3, ATOMS),
        in_specs=atoms_specs + [VMEM_ALL] * 4,
        out_specs=VMEM_ALL,
        scratch_shapes=[pltpu.VMEM((INNER + RIMS + 8, K), BF16)] * 2,
        compiler_params=params(2),
        cost_estimate=cost(2.0e10, 2**22),
        name="gather",
    )(*atoms, field, xr, yr, cr)


def solution(mesh):
    placed = (
        P(None, None, ("row", "col")),
        P(None, None, ("row", "col")),
        P(None, ("row", "col")),
        P(None, ("row", "col")),
        P("row", "col", None),
    )
    return jax.shard_map(
        shards, mesh=mesh, in_specs=placed, out_specs=P(None, None, ("row", "col")), check_vma=False
    )
```

profile of v0, /device:TPU:0, one launch (start us, length us, event | category | flops | bytes accessed | tf_op | source)
XLA Modules:
  0.0 139.8 jit_solution(6326007864452036589)
XLA Ops:
  0.0 1.5 %copy.22.cell_ref = s32[2,3,2048]{2,1,0:T(4,128)} copy(s32[2,3,2048]{2,0,1:T(2,128)} %param.17) | data formatting | bytes 98304 | tf_op args[0]
  1.5 0.7 copy.23.frac_ref
  2.1 0.6 copy.21.count_ref
  2.8 12.1 %spread.1 = (f32[4,512,128]{2,1,0:T(8,128)}, f32[4,80,128]{2,1,0:T(8,128)}, f32[4,160,128]{2,1,0:T(8,128)}, f32[4,40,128]{2,1,0:T(8,128)}) custom-call(s32[2,1]{1,0:T(2,128)} %copy.21.count_ref, s32[2,3,2048]{2,1,0:T(4,128)} %copy.22.cell_ref, f32[2,3,2048]{2,1,0:T(4,128)} %copy.23.frac_ref, f32[2,2048]{1,0:T(2,128)} %charge_ref.3), custom_call_target="tpu_custom_call" | custom-call | flops 10000000000 | bytes 2097152 | tf_op jit(solution)/shard_map/spread/pallas_call | solution.py:395
  14.9 5.0 %collective-permute-start.1 = (f32[4,160,128]{2,1,0:T(8,128)}, f32[4,160,128]{2,1,0:T(8,128)S(1)}, u32[]{:S(2)}, u32[]{:S(2)}) collective-permute-start(f32[4,160,128]{2,1,0:T(8,128)} %get-tuple-element.15), channel_id=1, source_target_pairs={{0,15},{1,0},{2,1},{3,2},{4,3},{5,4},{6,5},{7,6},{8,7},{9,8},{10,9... | collective-permute-start | bytes 983048 | tf_op jit(solution)/shard_map/ppermute | solution.py:363
  20.0 2.0 %green.1 = f32[512,256]{1,0:T(8,128)} custom-call(f32[512,256]{1,0:T(8,128)} %bitcast.12), custom_call_target="tpu_custom_call" | custom-call | flops 1000000 | bytes 1048576 | tf_op jit(solution)/shard_map/green/pallas_call | solution.py:377
  22.0 5.5 %all-to-all-start.1 = ((f32[8,64,256]{2,1,0:T(8,128)}), f32[8,64,256]{2,1,0:T(8,128)S(1)}, u32[]{:S(2)}, u32[]{:S(2)}) async-start(f32[8,64,256]{2,1,0:T(8,128)} %bitcast.7), calls=%async_computation.1 | async-start | bytes 1048576 | tf_op jit(solution)/shard_map/all_to_all | solution.py:387
  27.5 4.1 %collective-permute-start = (f32[4,80,128]{2,1,0:T(8,128)S(1)}, f32[4,80,128]{2,1,0:T(8,128)S(1)}, u32[]{:S(2)}, u32[]{:S(2)}) collective-permute-start(f32[4,80,128]{2,1,0:T(8,128)S(1)} %copy-done.4), channel_id=1, source_target_pairs={{0,112},{1,113},{2,114},{3,115},{4,116},{5,117},{6,118},{7,119},{8... | collective-permute-start | bytes 491528 | tf_op jit(solution)/shard_map/ppermute | solution.py:363
  31.6 4.7 %collective-permute-done.2.cr_ref = f32[4,40,128]{2,1,0:T(8,128)S(1)} collective-permute-done((f32[4,40,128]{2,1,0:T(8,128)S(1)}, f32[4,40,128]{2,1,0:T(8,128)S(1)}, u32[]{:S(2)}, u32[]{:S(2)}) %collective-permute-start.2) | collective-permute-done | bytes 81952 | tf_op jit(solution)/shard_map/ppermute | solution.py:363
  36.3 0.3 collective-permute-done.xr_ref
  36.7 0.3 copy-done.9
  37.0 0.3 copy-done.6
  37.5 4.0 %forward_z.1 = f32[2048,128]{1,0:T(8,128)} custom-call(f32[4,512,128]{2,1,0:T(8,128)} %get-tuple-element.13.mesh_ref, f32[4,80,128]{2,1,0:T(8,128)} %copy-done.6, f32[4,160,128]{2,1,0:T(8,128)} %copy-done.2, f32[4,40,128]{2,1,0:T(8,128)} %copy-done.9, bf16[256,256]{1,0:T(8,128)(2,1)} %constant.24.clone.ch, bf16[256,256]{1,0:T(8,128)(2,1)} %constant.25.clone.cl, ...), custom_call_target="tpu_custom_call" | custom-call | flops 2000000000 | bytes 4194304 | tf_op jit(solution)/shard_map/forward_z/pallas_call | solution.py:407
  41.5 28.6 %all_to_all.15 = f32[128,16,128]{2,1,0:T(8,128)} all-to-all(f32[128,16,128]{2,1,0:T(8,128)} %bitcast.10), channel_id=1, replica_groups=mesh['row'=8,'col'=16] {'row','col'}, dimensions={0} | all-to-all | bytes 2097152 | tf_op jit(solution)/shard_map/all_to_all | solution.py:367
  70.1 8.5 %planes.1 = f32[2048,128]{1,0:T(8,128)} custom-call(f32[2048,128]{1,0:T(8,128)} %bitcast.8, f32[512,256]{1,0:T(8,128)} %bitcast.13, bf16[512,512]{1,0:T(8,128)(2,1)} %constant.32.clone.eh, bf16[512,512]{1,0:T(8,128)(2,1)} %constant.33.clone.el, bf16[512,512]{1,0:T(8,128)(2,1)} %constant.34.clone.th, bf16[512,512]{1,0:T(8,128)(2,1)} %constant.35.clone.tl, ...), custom_call_target="tpu_custom_call" | custom-call | flops 4000000000 | bytes 8388608 | tf_op jit(solution)/shard_map/planes/pallas_call | solution.py:418
  78.6 24.5 %all_to_all.16 = f32[128,16,128]{2,1,0:T(8,128)} all-to-all(f32[128,16,128]{2,1,0:T(8,128)} %bitcast.9), channel_id=1, replica_groups=mesh['row'=8,'col'=16] {'row','col'}, dimensions={0} | all-to-all | bytes 2097152 | tf_op jit(solution)/shard_map/all_to_all | solution.py:367
  103.1 3.8 %inverse_z.1 = (f32[4,512,128]{2,1,0:T(8,128)}, f32[4,80,128]{2,1,0:T(8,128)}, f32[4,160,128]{2,1,0:T(8,128)}, f32[4,40,128]{2,1,0:T(8,128)}) custom-call(f32[2048,128]{1,0:T(8,128)} %bitcast.11, bf16[256,256]{1,0:T(8,128)(2,1)} %constant.24.clone.ch, bf16[256,256]{1,0:T(8,128)(2,1)} %constant.25.clone.cl, bf16[256,256]{1,0:T(8,128)(2,1)} %constant.26.clone.sh, ...), custom_call_target="tpu_custom_call" | custom-call | flops 2000000000 | bytes 4194304 | tf_op jit(solution)/shard_map/inverse_z/pallas_call | solution.py:429
  106.9 0.6 collective-permute-start.3
  107.5 2.2 %collective-permute-start.5 = (f32[4,40,128]{2,1,0:T(8,128)}, f32[4,40,128]{2,1,0:T(8,128)S(1)}, u32[]{:S(2)}, u32[]{:S(2)}) collective-permute-start(f32[4,40,128]{2,1,0:T(8,128)} %get-tuple-element.20), channel_id=1, source_target_pairs={{0,17},{1,18},{2,19},{3,20},{4,21},{5,22},{6,23},{7,24},{8,25},{9,... | collective-permute-start | bytes 245768 | tf_op jit(solution)/shard_map/ppermute | solution.py:363
  109.7 9.3 %collective-permute-done.5.cr_ref = f32[4,40,128]{2,1,0:T(8,128)S(1)} collective-permute-done((f32[4,40,128]{2,1,0:T(8,128)}, f32[4,40,128]{2,1,0:T(8,128)S(1)}, u32[]{:S(2)}, u32[]{:S(2)}) %collective-permute-start.5) | collective-permute-done | bytes 81952 | tf_op jit(solution)/shard_map/ppermute | solution.py:363
  119.0 0.6 copy-done.8
  119.6 0.2 copy-done.3
  119.8 18.5 %gather.1 = f32[2,3,2048]{2,1,0:T(4,128)} custom-call(s32[2,1]{1,0:T(2,128)} %copy.21.count_ref, s32[2,3,2048]{2,1,0:T(4,128)} %copy.22.cell_ref, f32[2,3,2048]{2,1,0:T(4,128)} %copy.23.frac_ref, f32[2,2048]{1,0:T(2,128)} %charge_ref.3, f32[4,512,128]{2,1,0:T(8,128)} %get-tuple-element.17.field_ref, f32[4,80,128]{2,1,0:T(8,128)} %copy-done.5, ...), custom_call_target="tpu_custom_call" | custom-call | flops 20000000000 | bytes 4194304 | tf_op jit(solution)/shard_map/gather/pallas_call | solution.py:439
  138.3 1.5 %copy.24 = f32[2,3,2048]{2,0,1:T(2,128)} copy(f32[2,3,2048]{2,1,0:T(4,128)} %gather.1) | data formatting | bytes 98304 | tf_op jit(solution)/shard_map/gather/pallas_call | solution.py:439
  (24 shorter events, 0.2 us)
Async XLA Ops:
  0.0 1.5 %copy-start.1 = (f32[2,3,2048]{2,0,1:T(2,128)S(1)}, f32[2,3,2048]{2,0,1:T(2,128)}, u32[]{:S(2)}) copy-start(f32[2,3,2048]{2,0,1:T(2,128)} %param.18) | copy-start | bytes 147460
  1.5 0.7 copy-start.10
  14.9 21.8 %collective-permute-start.1 = (f32[4,160,128]{2,1,0:T(8,128)}, f32[4,160,128]{2,1,0:T(8,128)S(1)}, u32[]{:S(2)}, u32[]{:S(2)}) collective-permute-start(f32[4,160,128]{2,1,0:T(8,128)} %get-tuple-element.15), channel_id=1, source_target_pairs={{0,15},{1,0},{2,1},{3,2},{4,3},{5,4},{6,5},{7,6},{8,7},{9,8},{10,9... | collective-permute-start | bytes 983048 | tf_op jit(solution)/shard_map/ppermute | solution.py:363
  22.0 5.5 %copy-start.4 = (f32[4,80,128]{2,1,0:T(8,128)S(1)}, f32[4,80,128]{2,1,0:T(8,128)}, u32[]{:S(2)}) copy-start(f32[4,80,128]{2,1,0:T(8,128)} %get-tuple-element.14) | copy-start | bytes 491524
  22.0 9.6 %copy-start.7 = (f32[4,40,128]{2,1,0:T(8,128)S(1)}, f32[4,40,128]{2,1,0:T(8,128)}, u32[]{:S(2)}) copy-start(f32[4,40,128]{2,1,0:T(8,128)} %get-tuple-element.16) | copy-start | bytes 245764
  22.0 19.5 %all-to-all-start.1 = ((f32[8,64,256]{2,1,0:T(8,128)}), f32[8,64,256]{2,1,0:T(8,128)S(1)}, u32[]{:S(2)}, u32[]{:S(2)}) async-start(f32[8,64,256]{2,1,0:T(8,128)} %bitcast.7), calls=%async_computation.1 | async-start | bytes 1048576 | tf_op jit(solution)/shard_map/all_to_all | solution.py:387
  27.5 9.2 %collective-permute-start = (f32[4,80,128]{2,1,0:T(8,128)S(1)}, f32[4,80,128]{2,1,0:T(8,128)S(1)}, u32[]{:S(2)}, u32[]{:S(2)}) collective-permute-start(f32[4,80,128]{2,1,0:T(8,128)S(1)} %copy-done.4), channel_id=1, source_target_pairs={{0,112},{1,113},{2,114},{3,115},{4,116},{5,117},{6,118},{7,119},{8... | collective-permute-start | bytes 491528 | tf_op jit(solution)/shard_map/ppermute | solution.py:363
  31.6 4.7 %collective-permute-start.2 = (f32[4,40,128]{2,1,0:T(8,128)S(1)}, f32[4,40,128]{2,1,0:T(8,128)S(1)}, u32[]{:S(2)}, u32[]{:S(2)}) collective-permute-start(f32[4,40,128]{2,1,0:T(8,128)S(1)} %copy-done.7), channel_id=1, source_target_pairs={{0,127},{1,112},{2,113},{3,114},{4,115},{5,116},{6,117},{7,118},{8... | collective-permute-start | bytes 245768 | tf_op jit(solution)/shard_map/ppermute | solution.py:363
  36.3 0.6 copy-start.9
  36.7 0.7 copy-start.6
  36.7 0.8 copy-start.2
  41.5 28.6 %copy-start = (f32[8,64,256]{2,1,0:T(8,128)}, f32[8,64,256]{2,1,0:T(8,128)S(1)}, u32[]{:S(2)}) copy-start(f32[8,64,256]{2,1,0:T(8,128)S(1)} %all-to-all-done.1) | copy-start | bytes 1572868
  106.9 12.1 %collective-permute-start.4 = (f32[4,160,128]{2,1,0:T(8,128)}, f32[4,160,128]{2,1,0:T(8,128)S(1)}, u32[]{:S(2)}, u32[]{:S(2)}) collective-permute-start(f32[4,160,128]{2,1,0:T(8,128)} %get-tuple-element.19), channel_id=1, source_target_pairs={{0,1},{1,2},{2,3},{3,4},{4,5},{5,6},{6,7},{7,8},{8,9},{9,10},{10,1... | collective-permute-start | bytes 983048 | tf_op jit(solution)/shard_map/ppermute | solution.py:363
  106.9 12.1 %collective-permute-start.3 = (f32[4,80,128]{2,1,0:T(8,128)}, f32[4,80,128]{2,1,0:T(8,128)S(1)}, u32[]{:S(2)}, u32[]{:S(2)}) collective-permute-start(f32[4,80,128]{2,1,0:T(8,128)} %get-tuple-element.18), channel_id=1, source_target_pairs={{0,16},{1,17},{2,18},{3,19},{4,20},{5,21},{6,22},{7,23},{8,24},{9,... | collective-permute-start | bytes 491528 | tf_op jit(solution)/shard_map/ppermute | solution.py:363
  107.5 11.5 %collective-permute-start.5 = (f32[4,40,128]{2,1,0:T(8,128)}, f32[4,40,128]{2,1,0:T(8,128)S(1)}, u32[]{:S(2)}, u32[]{:S(2)}) collective-permute-start(f32[4,40,128]{2,1,0:T(8,128)} %get-tuple-element.20), channel_id=1, source_target_pairs={{0,17},{1,18},{2,19},{3,20},{4,21},{5,22},{6,23},{7,24},{8,25},{9,... | collective-permute-start | bytes 245768 | tf_op jit(solution)/shard_map/ppermute | solution.py:363
  118.9 0.6 copy-start.8
  118.9 0.7 copy-start.5
  119.0 0.8 copy-start.3
where the time goes:
time: 141 us; the launch traced here: 140 us
  blocking collectives  53.1 us (38%)
  Pallas kernels  49 us (35%)
  starting transfers between devices  17.4 us (12%)
  waiting for transfers between devices  14.3 us (10%)
  local copies, waits for them, and re-layouts  5.91 us (4%)
    all_to_all x2, blocking collectives, everywhere(): lax.all_to_all(value, ('row', 'col'), split_axis=0, concat_axis=0, tiled=...  53.1 us
    pallas_call x1, Pallas kernels, shards(): pl.pallas_call(gather_kernel, grid=(2, steps), out_shape=shape(2, 3, ATOM...  18.5 us
    ppermute x6, waiting for transfers between devices, shift(): return lax.ppermute(value, ('row', 'col'), pairs)  14.3 us
    pallas_call x1, Pallas kernels, shards(): pl.pallas_call(spread_kernel, grid=(2, steps), out_shape=[shape(4, INNER,...  12.1 us
    ppermute x6, starting transfers between devices, shift(): return lax.ppermute(value, ('row', 'col'), pairs)  12 us
    pallas_call x1, Pallas kernels, shards(): pl.pallas_call(plane_kernel, out_shape=shape(DEV * 16, 128), in_specs=[VM...  8.51 us
    all_to_all x1, starting transfers between devices, shards(): lax.all_to_all(green.reshape(ROWS, 64, K), 'row', split_axis=0, concat_ax...  5.47 us
    unnamed x25, local copies, waits for them, and re-layouts  4.42 us
  transfers between devices with their start and end apart: 7, of which 3 were waited for; matrix products, arithmetic and copies ran while one was open for 0% of the time, Pallas kernels for 4%

commit v1 on v0

v1 whole, which is shorter than its diff:
```python
import math

import jax
import jax.numpy as jnp
import numpy as np
from jax import lax
from jax.experimental import pallas as pl
from jax.experimental.pallas import tpu as pltpu
from jax.sharding import PartitionSpec as P

F32 = jnp.float32
BF16 = jnp.bfloat16
K = 256
XB = 32
YB = 16
ROWS = 8
COLS = 16
DEV = ROWS * COLS
ATOMS = 2048
CHUNK = 256
RIM = 5
INNER = XB * YB
XRIM = RIM * YB
YRIM = RIM * XB
CRIM = RIM * 8
RIMS = XRIM + YRIM + CRIM
VMEM_ALL = pl.BlockSpec(memory_space=pltpu.VMEM)
SMEM_ALL = pl.BlockSpec(memory_space=pltpu.SMEM)


def halves(values):
    top = values.astype(np.float32).astype(jnp.bfloat16)
    rest = (values - top.astype(np.float64)).astype(np.float32).astype(jnp.bfloat16)
    return top, rest


def z_tables():
    p, d = np.meshgrid(np.arange(2), np.arange(DEV), indexing="ij")
    kz = (16 * (d % COLS) + 2 * (d // COLS) + p).reshape(-1)
    angle = 2.0 * math.pi * ((kz[:, None] * np.arange(K)[None, :]) % K) / K
    return np.stack(halves(np.cos(angle)) + halves(np.sin(angle)))


def x_tables():
    x = np.arange(K)
    angle = 2.0 * math.pi * ((x[:, None] * x[None, :]) % K) / K
    return np.stack(halves(np.cos(angle)) + halves(np.sin(angle)))


def y_table():
    c, low, part, high = np.meshgrid(
        np.arange(COLS), np.arange(4), np.arange(2), np.arange(4), indexing="ij"
    )
    y = (16 * c + 4 * high + low).reshape(-1)
    part = part.reshape(-1)[None, :]
    angle = 2.0 * math.pi * ((np.arange(K)[:, None] * y[None, :]) % K) / K
    cosine, sine = np.cos(angle), np.sin(angle)
    real = np.where(part == 0, cosine, sine)
    imag = np.where(part == 0, -sine, cosine)
    return np.concatenate([real, imag], axis=0)


def split(value):
    top = value.astype(BF16)
    return top, (value - top.astype(F32)).astype(BF16)


def dot(a, b, dims=((1,), (0,))):
    return lax.dot_general(a, b, (dims, ((), ())), preferred_element_type=F32)


def dot3(a, b, dims=((1,), (0,))):
    return dot(a[0], b[0], dims) + dot(a[0], b[1], dims) + dot(a[1], b[0], dims)


def spline_values(fraction):
    nothing = jnp.zeros_like(fraction)
    levels = [fraction, 1.0 - fraction]
    slopes = levels
    for degree in range(3, 7):
        padded = levels + [nothing]
        following = []
        for offset in range(degree):
            beneath = padded[offset - 1] if offset > 0 else nothing
            following.append(
                ((fraction + offset) * padded[offset] + (degree - fraction - offset) * beneath)
                * (1.0 / (degree - 1))
            )
        if degree == 6:
            slopes = [
                padded[offset] - (padded[offset - 1] if offset > 0 else nothing)
                for offset in range(6)
            ]
        levels = following
    return levels, slopes


def placed_rows(cell, values, first, count, wrapped):
    shape = (count, cell.shape[1])
    behind = cell - (lax.broadcasted_iota(jnp.int32, shape, 0) + first)
    if wrapped:
        behind = behind & (K - 1)
    masks = [behind == j for j in range(6)]
    results = []
    for value in values:
        total = jnp.zeros(shape, F32)
        for j in range(6):
            total = jnp.where(masks[j], value[j], total)
        results.append(total)
    return results


def atom_rows(frac_ref, lanes):
    fraction = jnp.concatenate([frac_ref[d, :, lanes] for d in range(3)], axis=0)
    return spline_values(fraction)


def live_charges(charge_ref, count_ref, s, at, lanes):
    slots = lax.broadcasted_iota(jnp.int32, (1, lanes.size), 1) + at
    return jnp.where(slots < count_ref[0, s], charge_ref[s : s + 1, lanes], 0.0)


def pick(rows, d, s):
    return [w[2 * d + s : 2 * d + s + 1] for w in rows]


def plane_rows(cell_ref, tables, s, lanes):
    first = cell_ref[0, s : s + 1, lanes] & (XB - 1)
    second = cell_ref[1, s : s + 1, lanes] & (YB - 1)
    return (
        placed_rows(first, [pick(t, 0, s) for t in tables], -8, XB + 8, False),
        placed_rows(second, [pick(t, 1, s) for t in tables], -8, YB + 8, False),
    )


def put(ph, pq, at, product):
    top, rest = split(product)
    ph[at : at + product.shape[0], :] = top
    pq[at : at + product.shape[0], :] = rest


ALL = pl.ds(0, ATOMS)


def give(total, s, pieces):
    for ref, at, count in pieces:
        for h in range(2):
            ref[2 * s + h] = total[at : at + count, h * 128 : h * 128 + 128]


def spread_rim_kernel(
    count_ref, cell_hbm, frac_hbm, charge_hbm, xr_ref, yr_ref, cr_ref, wh_ref, wl_ref,
    cell_ref, frac_ref, charge_ref, ph, pq, sems,
):
    copies = [
        pltpu.make_async_copy(source, target, sems.at[n])
        for n, (source, target) in enumerate(
            ((cell_hbm, cell_ref), (frac_hbm, frac_ref), (charge_hbm, charge_ref))
        )
    ]
    for copy in copies:
        copy.start()
    for copy in copies:
        copy.wait()
    levels, _ = atom_rows(frac_ref, ALL)
    for s in range(2):
        (first,), (second,) = plane_rows(cell_ref, [levels], s, ALL)
        (third,) = placed_rows(cell_ref[2, s : s + 1, :], [pick(levels, 2, s)], 0, K, True)
        wh_ref[s], wl_ref[s] = split(third)
        second = second * live_charges(charge_ref, count_ref, s, 0, ALL)
        p, q = ph.at[s], pq.at[s]
        for x in range(RIM):
            put(p, q, x * YB, first[3 + x : 4 + x] * second[8:])
        for y in range(RIM):
            put(p, q, XRIM + y * XB, second[3 + y : 4 + y] * first[8:])
        corner = [second[3 + y : 4 + y] * first[:8] for y in range(RIM)]
        corner.append(jnp.zeros((8, ATOMS), F32))
        for y in range(0, RIM + 1, 2):
            put(p, q, XRIM + YRIM + y * 8, jnp.concatenate(corner[y : y + 2], axis=0))
        total = dot3((p[...], q[...]), (wh_ref[s], wl_ref[s]), ((1,), (1,)))
        give(total, s, ((xr_ref, 0, XRIM), (yr_ref, XRIM, YRIM), (cr_ref, XRIM + YRIM, CRIM)))


def spread_kernel(count_ref, cell_ref, frac_ref, charge_ref, wh_ref, wl_ref, mesh_ref, ph, pq):
    levels, _ = atom_rows(frac_ref, ALL)
    for s in range(2):
        (first,), (second,) = plane_rows(cell_ref, [levels], s, ALL)
        second = second * live_charges(charge_ref, count_ref, s, 0, ALL)
        p, q = ph.at[s], pq.at[s]
        for y in range(YB):
            put(p, q, y * XB, second[8 + y : 9 + y] * first[8:])
        total = dot3((p[...], q[...]), (wh_ref[s], wl_ref[s]), ((1,), (1,)))
        give(total, s, ((mesh_ref, 0, INNER),))


def weight_kernel(cell_ref, frac_ref, wh_ref, wl_ref, sh_ref, sl_ref):
    levels, slopes = atom_rows(frac_ref, ALL)
    for s in range(2):
        value, slope = placed_rows(
            cell_ref[2, s : s + 1, :], [pick(levels, 2, s), pick(slopes, 2, s)], 0, K, True
        )
        wh_ref[s], wl_ref[s] = split(value)
        sh_ref[s], sl_ref[s] = split(slope)


def forward_z_kernel(mesh_ref, xr_ref, yr_ref, cr_ref, zc, out_ref, m):
    m[...] = mesh_ref[...]
    parts = []
    for s in range(2):
        base = (YB - RIM) * XB
        columns = []
        for h in range(2):
            k = 2 * s + h
            m[k, base : base + YRIM, :] += yr_ref[k]
            for x in range(RIM):
                rows = pl.ds(XB - RIM + x, YB, stride=XB)
                m[k, rows, :] += xr_ref[k, x * YB : x * YB + YB, :]
            for y in range(RIM):
                at = (YB - RIM + y) * XB + XB - 8
                m[k, at : at + 8, :] += cr_ref[k, y * 8 : y * 8 + 8]
            columns.append(m[k].T)
        parts.append(split(jnp.concatenate(columns, axis=0)))
    cosines, sines = (zc[0], zc[1]), (zc[2], zc[3])
    real = dot3(cosines, parts[0]) + dot3(sines, parts[1])
    imag = dot3(cosines, parts[1]) - dot3(sines, parts[0])
    for q, value in enumerate((real, imag)):
        for p in range(2):
            for b in range(4):
                out_ref[pl.ds(p * 8 + q * 4 + b, DEV, stride=16), :] = value[
                    p * DEV : (p + 1) * DEV, b * 128 : (b + 1) * 128
                ]


def exchange_blocks(pieces):
    lane = lax.broadcasted_iota(jnp.int32, pieces[0].shape, 1)
    for bit in (1, 2):
        upper = (lane // 32) & bit == bit
        fresh = list(pieces)
        for v in range(4):
            if v & bit == 0:
                a, b = pieces[v], pieces[v | bit]
                fresh[v] = jnp.where(upper, pltpu.roll(b, 32 * bit, 1), a)
                fresh[v | bit] = jnp.where(upper, b, pltpu.roll(a, 128 - 32 * bit, 1))
        pieces = fresh
    return pieces


def plane_kernel(buf_ref, green_ref, yc, xc, out_ref, d, o):
    cosines, sines = (xc[0], xc[1]), (xc[2], xc[3])
    for p in range(2):
        for c in range(COLS):
            for g in range(2):
                tiles = []
                for r in range(4):
                    at = ((g * 4 + r) * COLS + c) * 16 + p * 8
                    tiles.append(buf_ref[at : at + 8, :])
                for low, tile in enumerate(exchange_blocks(tiles)):
                    at = (c * 4 + low) * 8
                    d[at : at + 8, g * 128 : g * 128 + 128] = tile
        first = dot3((yc[0], yc[1]), split(d[...]))
        real, imag = split(first[:K]), split(first[K:])
        f_real = dot3(real, cosines) + dot3(imag, sines)
        f_imag = dot3(imag, cosines) - dot3(real, sines)
        green = jnp.concatenate(
            [green_ref[(r * 2 + p) * XB : (r * 2 + p + 1) * XB, :] for r in range(ROWS)], axis=0
        ) * (1.0 / float(K) ** 3)
        real, imag = split(f_real * green), split(f_imag * green)
        t_real = split(dot3(real, cosines) - dot3(imag, sines))
        t_imag = split(dot3(imag, cosines) + dot3(real, sines))
        both = tuple(jnp.concatenate([a, b], axis=0) for a, b in zip(t_real, t_imag))
        o[...] = dot3((yc[2], yc[3]), both)
        for c in range(COLS):
            for g in range(2):
                tiles = []
                for low in range(4):
                    at = (c * 4 + low) * 8
                    tiles.append(o[at : at + 8, g * 128 : g * 128 + 128])
                for r, tile in enumerate(exchange_blocks(tiles)):
                    at = ((g * 4 + r) * COLS + c) * 16 + p * 8
                    out_ref[at : at + 8, :] = tile


def inverse_z_kernel(buf_ref, zc, fh_ref, fl_ref, xr_ref, yr_ref, cr_ref, m):
    cosines, sines = (zc[0], zc[1]), (zc[2], zc[3])
    parts = []
    for q in range(2):
        columns = []
        for p in range(2):
            blocks = []
            for b in range(4):
                blocks.append(buf_ref[pl.ds(p * 8 + q * 4 + b, DEV, stride=16), :].T)
            columns.append(jnp.concatenate(blocks, axis=0))
        parts.append(split(jnp.concatenate(columns, axis=1)))
    real, imag = parts
    fields = (
        dot3(real, cosines) - dot3(imag, sines),
        dot3(imag, cosines) + dot3(real, sines),
    )
    base = (YB - RIM) * XB
    for s in range(2):
        fh_ref[s], fl_ref[s] = split(fields[s])
        for h in range(2):
            k = 2 * s + h
            m[k] = fields[s][:, h * 128 : h * 128 + 128]
            yr_ref[k] = m[k, base : base + YRIM, :]
            for x in range(RIM):
                rows = pl.ds(XB - RIM + x, YB, stride=XB)
                xr_ref[k, x * YB : x * YB + YB, :] = m[k, rows, :]
            for y in range(RIM):
                at = (YB - RIM + y) * XB + XB - 8
                cr_ref[k, y * 8 : y * 8 + 8, :] = m[k, at : at + 8, :]


def row(pair, n):
    return pair[0][n : n + 1], pair[1][n : n + 1]


def weighed(plain, sloped, at, along, across):
    value, slope = across
    size = value.shape[0]
    sums = [None] * 3
    for n, (mine, mine_slope) in enumerate(along):
        rows = slice(at + n * size, at + (n + 1) * size)
        terms = (mine * plain[rows], mine_slope * plain[rows], mine * sloped[rows])
        sums = [term if n == 0 else old + term for old, term in zip(sums, terms)]
    return tuple(
        jnp.sum(total * side, axis=0, keepdims=True)
        for total, side in zip(sums, (slope, value, value))
    )


def chunks(body):
    def step(i, carry):
        at = pl.multiple_of(i * CHUNK, CHUNK)
        body(at, pl.ds(at, CHUNK))
        return carry

    lax.fori_loop(0, ATOMS // CHUNK, step, 0)


def gather_kernel(cell_ref, frac_ref, wh_ref, wl_ref, sh_ref, sl_ref, fh_ref, fl_ref, out_ref):
    def body(at, lanes):
        tables = atom_rows(frac_ref, lanes)
        for s in range(2):
            xs, ys = plane_rows(cell_ref, tables, s, lanes)
            field = fh_ref[s], fl_ref[s]
            plain = dot3(field, (wh_ref[s, :, lanes], wl_ref[s, :, lanes]))
            sloped = dot3(field, (sh_ref[s, :, lanes], sl_ref[s, :, lanes]))
            lines = [row(ys, 8 + y) for y in range(YB)]
            forces = weighed(plain, sloped, 0, lines, (xs[0][8:], xs[1][8:]))
            for d in range(3):
                out_ref[d, s : s + 1, lanes] = forces[d]

    chunks(body)


def gather_rim_kernel(
    count_ref, cell_ref, frac_ref, charge_ref, wh_ref, wl_ref, sh_ref, sl_ref,
    xr_ref, yr_ref, cr_ref, inner_ref, out_ref, fh, fl,
):
    for s in range(2):
        for h in range(2):
            k, columns = 2 * s + h, slice(h * 128, h * 128 + 128)
            corner = jnp.concatenate([cr_ref[k], jnp.zeros((8, 128), F32)], axis=0)
            for value, at in ((xr_ref[k], 0), (yr_ref[k], XRIM), (corner, XRIM + YRIM)):
                top, rest = split(value)
                fh[s, at : at + value.shape[0], columns] = top
                fl[s, at : at + value.shape[0], columns] = rest

    def body(at, lanes):
        tables = atom_rows(frac_ref, lanes)
        for s in range(2):
            xs, ys = plane_rows(cell_ref, tables, s, lanes)
            field = fh[s], fl[s]
            plain = dot3(field, (wh_ref[s, :, lanes], wl_ref[s, :, lanes]))
            sloped = dot3(field, (sh_ref[s, :, lanes], sl_ref[s, :, lanes]))
            lines = [row(ys, 3 + y) for y in range(RIM)]
            columns = [row(xs, 3 + x) for x in range(RIM)]
            side = weighed(plain, sloped, 0, columns, (ys[0][8:], ys[1][8:]))
            edge = weighed(plain, sloped, XRIM, lines, (xs[0][8:], xs[1][8:]))
            corner = weighed(plain, sloped, XRIM + YRIM, lines, (xs[0][:8], xs[1][:8]))
            charges = live_charges(charge_ref, count_ref, s, at, lanes)
            for d, e in ((0, 1), (1, 0), (2, 2)):
                force = inner_ref[d, s : s + 1, lanes] + side[e] + edge[d] + corner[d]
                out_ref[d, s : s + 1, lanes] = -charges * force

    chunks(body)


def green_kernel(in_ref, out_ref, m):
    for h in range(2):
        lanes = slice(h * 128, h * 128 + 128)
        m[...] = in_ref[:, lanes]
        for k in range(COLS):
            out_ref[k * XB : (k + 1) * XB, lanes] = m[pl.ds(k, XB, stride=COLS), :]


def call(kernel, name, flops, out_shape, operands, smem=(), hbm=(), scratch=(), limit=24):
    def spec(n):
        if n in hbm:
            return pl.BlockSpec(memory_space=pltpu.HBM)
        return SMEM_ALL if n in smem else VMEM_ALL

    single = not isinstance(out_shape, list)
    shapes = [out_shape] if single else out_shape
    size = sum(math.prod(v.shape) * v.dtype.itemsize for v in list(operands) + shapes)
    return pl.pallas_call(
        kernel,
        out_shape=out_shape,
        in_specs=[spec(n) for n in range(len(operands))],
        out_specs=VMEM_ALL if single else [VMEM_ALL] * len(shapes),
        scratch_shapes=list(scratch),
        compiler_params=pltpu.CompilerParams(vmem_limit_bytes=limit * 2**20),
        cost_estimate=pl.CostEstimate(flops=int(flops), bytes_accessed=size, transcendentals=0),
        name=name,
    )(*operands)


def shape(*dims, dtype=F32):
    return jax.ShapeDtypeStruct(dims, dtype)


def shift(value, rows, cols):
    pairs = []
    for r in range(ROWS):
        for c in range(COLS):
            pairs.append((r * COLS + c, ((r + rows) % ROWS) * COLS + (c + cols) % COLS))
    return lax.ppermute(value, ("row", "col"), pairs)


def everywhere(value):
    return lax.all_to_all(value, ("row", "col"), split_axis=0, concat_axis=0, tiled=True)


def shards(cell_index, fraction, charge, atom_count, influence):
    zc = jnp.asarray(z_tables())
    xc = jnp.asarray(x_tables())
    table = y_table()
    yc = jnp.asarray(np.stack(halves(table) + halves(np.ascontiguousarray(table.T))))

    cells = jnp.transpose(cell_index, (1, 0, 2))
    fractions = jnp.transpose(fraction, (1, 0, 2))
    counts = jnp.transpose(atom_count, (1, 0))
    atoms = (counts, cells, fractions, charge)
    rim_shapes = [shape(4, XRIM, 128), shape(4, YRIM, 128), shape(4, CRIM, 128)]
    weights = shape(2, K, ATOMS, dtype=BF16)

    xr, yr, cr, wh, wl = call(
        spread_rim_kernel, "spread_rim", 6e9, rim_shapes + [weights] * 2, atoms,
        smem=(0,), hbm=(1, 2, 3),
        scratch=[
            pltpu.VMEM((3, 2, ATOMS), jnp.int32),
            pltpu.VMEM((3, 2, ATOMS), F32),
            pltpu.VMEM((2, ATOMS), F32),
            pltpu.VMEM((2, RIMS + 8, ATOMS), BF16),
            pltpu.VMEM((2, RIMS + 8, ATOMS), BF16),
            pltpu.SemaphoreType.DMA((3,)),
        ],
    )
    xr, yr, cr = shift(xr, -1, 0), shift(yr, 0, -1), shift(cr, -1, -1)
    green = call(
        green_kernel, "green", 1e8, shape(512, K), (influence.reshape(XB * COLS, K),),
        scratch=[pltpu.VMEM((512, 128), F32)],
    )
    green = lax.all_to_all(
        green.reshape(ROWS, 64, K), "row", split_axis=0, concat_axis=0, tiled=True
    ).reshape(512, K)
    mesh = call(
        spread_kernel, "spread", 8e9, shape(4, INNER, 128), atoms + (wh, wl),
        smem=(0,),
        scratch=[pltpu.VMEM((2, INNER, ATOMS), BF16)] * 2,
    )
    packed = call(
        forward_z_kernel, "forward_z", 3e9, shape(DEV * 16, 128), (mesh, xr, yr, cr, zc),
        scratch=[pltpu.VMEM((4, INNER, 128), F32)],
    )
    packed = everywhere(packed.reshape(DEV, 16, 128)).reshape(DEV * 16, 128)
    wh, wl, gh, gl = call(weight_kernel, "weights", 1e10, [weights] * 4, (cells, fractions))
    packed = call(
        plane_kernel, "planes", 6e9, shape(DEV * 16, 128), (packed, green, yc, xc),
        scratch=[pltpu.VMEM((512, K), F32)] * 2,
    )
    packed = everywhere(packed.reshape(DEV, 16, 128)).reshape(DEV * 16, 128)
    fh, fl, xr, yr, cr = call(
        inverse_z_kernel, "inverse_z", 3e9, [shape(2, INNER, K, dtype=BF16)] * 2 + rim_shapes,
        (packed, zc),
        scratch=[pltpu.VMEM((4, INNER, 128), F32)],
    )
    xr, yr, cr = shift(xr, 1, 0), shift(yr, 0, 1), shift(cr, 1, 1)
    inner = call(
        gather_kernel, "gather", 1.2e10, shape(3, 2, ATOMS),
        (cells, fractions, wh, wl, gh, gl, fh, fl),
    )
    forces = call(
        gather_rim_kernel, "gather_rim", 8e9, shape(3, 2, ATOMS),
        atoms + (wh, wl, gh, gl, xr, yr, cr, inner), smem=(0,),
        scratch=[pltpu.VMEM((2, RIMS + 8, K), BF16)] * 2,
    )
    return jnp.transpose(forces, (1, 0, 2))


def solution(mesh):
    placed = (
        P(None, None, ("row", "col")),
        P(None, None, ("row", "col")),
        P(None, ("row", "col")),
        P(None, ("row", "col")),
        P("row", "col", None),
    )
    return jax.shard_map(
        shards, mesh=mesh, in_specs=placed, out_specs=P(None, None, ("row", "col")), check_vma=False
    )
```

time: 141 us -> 108 us (0.77)
  blocking collectives: 53.1 us -> 27 us
  Pallas kernels: 49 us -> 40.5 us
  starting transfers between devices: 17.4 us -> 21.5 us
  waiting for transfers between devices: 14.3 us -> 11.3 us
  local copies, waits for them, and re-layouts: 5.91 us -> 7.47 us
    all_to_all x2 -> x1, blocking collectives: 53.1 us -> 27 us  [everywhere(): lax.all_to_all(value, ('row', 'col'), split_axis=0, concat_axis=0, tiled=...]
    ppermute x6, waiting for transfers between devices: 14.3 us -> 2.85 us  [shift(): return lax.ppermute(value, ('row', 'col'), pairs)]
    pallas_call x6 -> x9, Pallas kernels: 49 us -> 40.5 us  [call(): pl.pallas_call(kernel, out_shape=out_shape, in_specs=[spec(n) for n in ra...]
    all_to_all x0 -> x1, waiting for transfers between devices: none -> 8.46 us  [everywhere(): lax.all_to_all(value, ('row', 'col'), split_axis=0, concat_axis=0, tiled=...]
    all_to_all x0 -> x1, starting transfers between devices: none -> 4.63 us  [everywhere(): lax.all_to_all(value, ('row', 'col'), split_axis=0, concat_axis=0, tiled=...]
    unnamed x25 -> x32, local copies, waits for them, and re-layouts: 4.42 us -> 7.47 us
    pallas_call x1 -> x0, local copies, waits for them, and re-layouts: 1.5 us -> none  [shards(): pl.pallas_call(gather_kernel, grid=(2, steps), out_shape=shape(2, 3, ATOM...]
  transfers between devices with their start and end apart: 7 -> 8, of which waited for: 3 -> 3; matrix products, arithmetic and copies ran while one was open for 0% -> 0% of each run, Pallas kernels for 4% -> 23%
where the time goes in v1:
time: 108 us
  Pallas kernels  40.5 us (38%)
  blocking collectives  27 us (25%)
  starting transfers between devices  21.5 us (20%)
  waiting for transfers between devices  11.3 us (10%)
  local copies, waits for them, and re-layouts  7.47 us (7%)
    pallas_call x9, Pallas kernels, call(): pl.pallas_call(kernel, out_shape=out_shape, in_specs=[spec(n) for n in ra...  40.5 us
    all_to_all x1, blocking collectives, everywhere(): lax.all_to_all(value, ('row', 'col'), split_axis=0, concat_axis=0, tiled=...  27 us
    ppermute x6, starting transfers between devices, shift(): return lax.ppermute(value, ('row', 'col'), pairs)  10.6 us
    all_to_all x1, waiting for transfers between devices, everywhere(): lax.all_to_all(value, ('row', 'col'), split_axis=0, concat_axis=0, tiled=...  8.46 us
    unnamed x32, local copies, waits for them, and re-layouts  7.47 us
    all_to_all x1, starting transfers between devices, shards(): lax.all_to_all(green.reshape(ROWS, 64, K), 'row', split_axis=0, concat_ax...  6.35 us
    all_to_all x1, starting transfers between devices, everywhere(): lax.all_to_all(value, ('row', 'col'), split_axis=0, concat_axis=0, tiled=...  4.63 us
    ppermute x6, waiting for transfers between devices, shift(): return lax.ppermute(value, ('row', 'col'), pairs)  2.85 us
  transfers between devices with their start and end apart: 8, of which 3 were waited for; matrix products, arithmetic and copies ran while one was open for 0% of the time, Pallas kernels for 23%

profile of v1, /device:TPU:0, one launch (start us, length us, event | category | flops | bytes accessed | tf_op | source)
XLA Modules:
  0.0 107.9 jit_solution(10386759746475927089)
XLA Ops:
  0.0 1.1 copy-done
  1.1 1.0 green.1
  2.1 6.4 %all-to-all-start.1 = ((f32[8,64,256]{2,1,0:T(8,128)}), f32[8,64,256]{2,1,0:T(8,128)S(1)}, u32[]{:S(2)}, u32[]{:S(2)}) async-start(f32[8,64,256]{2,1,0:T(8,128)} %bitcast.6), calls=%async_computation.1 | async-start | bytes 1048576 | tf_op jit(solution)/shard_map/all_to_all | solution.py:465
  8.5 5.9 %spread_rim.1 = (f32[4,80,128]{2,1,0:T(8,128)S(1)}, f32[4,160,128]{2,1,0:T(8,128)S(1)}, f32[4,40,128]{2,1,0:T(8,128)S(1)}, bf16[2,256,2048]{2,1,0:T(8,128)(2,1)S(1)}, bf16[2,256,2048]{2,1,0:T(8,128)(2,1)S(1)}) custom-call(s32[1,2]{1,0:T(1,128)S(1)} %bitcast.26, s32[3,2,2048]{2,1,0:T(2,128)S(1)} %bitcast.16, f32[3,2,2048]{2,1,0:T(2,128)S(1)} %bitcast.21, ...), custom_call_target="tpu_custom_call" | custom-call | flops 6000000000 | bytes 4882440 | tf_op jit(solution)/shard_map/spread_rim/pallas_call | solution.py:407
  14.3 6.8 %collective-permute-start.2 = (f32[4,40,128]{2,1,0:T(8,128)S(1)}, f32[4,40,128]{2,1,0:T(8,128)S(1)}, u32[]{:S(2)}, u32[]{:S(2)}) collective-permute-start(f32[4,40,128]{2,1,0:T(8,128)S(1)} %get-tuple-element.27), channel_id=1, source_target_pairs={{0,127},{1,112},{2,113},{3,114},{4,115},{5,116},{6,117},{7,118},{8... | collective-permute-start | bytes 245768 | tf_op jit(solution)/shard_map/ppermute | solution.py:428
  21.1 2.6 %collective-permute-start.1 = (f32[4,160,128]{2,1,0:T(8,128)S(1)}, f32[4,160,128]{2,1,0:T(8,128)S(1)}, u32[]{:S(2)}, u32[]{:S(2)}) collective-permute-start(f32[4,160,128]{2,1,0:T(8,128)S(1)} %get-tuple-element.26), channel_id=1, source_target_pairs={{0,15},{1,0},{2,1},{3,2},{4,3},{5,4},{6,5},{7,6},{8,7},{9,8},{10,9... | collective-permute-start | bytes 983048 | tf_op jit(solution)/shard_map/ppermute | solution.py:428
  23.7 4.4 %spread.1.mesh_ref = f32[4,512,128]{2,1,0:T(8,128)S(1)} custom-call(s32[1,2]{1,0:T(1,128)S(1)} %bitcast.27, s32[3,2,2048]{2,1,0:T(2,128)S(1)} %bitcast.17, f32[3,2,2048]{2,1,0:T(2,128)S(1)} %bitcast.22, f32[2,2048]{1,0:T(2,128)S(1)} %copy-done.3, bf16[2,256,2048]{2,1,0:T(8,128)(2,1)S(1)} %get-tuple-element.23.wh_ref, ...), custom_call_target="tpu_custom_call" | custom-call | flops 8000000000 | bytes 5357576 | tf_op jit(solution)/shard_map/spread/pallas_call | solution.py:407
  28.3 1.5 %forward_z.1 = f32[2048,128]{1,0:T(8,128)S(1)} custom-call(f32[4,512,128]{2,1,0:T(8,128)S(1)} %spread.1.mesh_ref, f32[4,80,128]{2,1,0:T(8,128)S(1)} %collective-permute-done.xr_ref, f32[4,160,128]{2,1,0:T(8,128)S(1)} %collective-permute-done.1.yr_ref, f32[4,40,128]{2,1,0:T(8,128)S(1)} %collective-permute-done.2.cr_ref, bf16[4,256,256]{2,1,0:T(8,128)(2,1)S(1)} %copy-done.6), custom_call_target="tpu_custom_call" | custom-call | flops 3000000000 | bytes 3194880 | tf_op jit(solution)/shard_map/forward_z/pallas_call | solution.py:407
  29.8 27.0 %all_to_all.15 = f32[128,16,128]{2,1,0:T(8,128)S(1)} all-to-all(f32[128,16,128]{2,1,0:T(8,128)S(1)} %bitcast.12), channel_id=1, replica_groups=mesh['row'=8,'col'=16] {'row','col'}, dimensions={0} | all-to-all | bytes 2097152 | tf_op jit(solution)/shard_map/all_to_all | solution.py:432
  56.8 6.5 %planes.1 = f32[2048,128]{1,0:T(8,128)} custom-call(f32[2048,128]{1,0:T(8,128)S(1)} %bitcast.13, f32[512,256]{1,0:T(8,128)S(1)} %bitcast.15, bf16[4,512,512]{2,1,0:T(8,128)(2,1)S(1)} %copy-done.5, bf16[4,256,256]{2,1,0:T(8,128)(2,1)S(1)} %copy-done.7), custom_call_target="tpu_custom_call" | custom-call | flops 6000000000 | bytes 5242880 | tf_op jit(solution)/shard_map/planes/pallas_call | solution.py:407
  63.3 4.6 %all-to-all-start.2 = ((f32[128,16,128]{2,1,0:T(8,128)}), f32[128,16,128]{2,1,0:T(8,128)S(1)}, u32[]{:S(2)}, u32[]{:S(2)}) async-start(f32[128,16,128]{2,1,0:T(8,128)} %bitcast.8), calls=%async_computation.2 | async-start | bytes 2097152 | tf_op jit(solution)/shard_map/all_to_all | solution.py:432
  67.9 5.1 %weights.1 = (bf16[2,256,2048]{2,1,0:T(8,128)(2,1)S(1)}, bf16[2,256,2048]{2,1,0:T(8,128)(2,1)S(1)}, bf16[2,256,2048]{2,1,0:T(8,128)(2,1)S(1)}, bf16[2,256,2048]{2,1,0:T(8,128)(2,1)S(1)}) custom-call(s32[3,2,2048]{2,1,0:T(2,128)S(1)} %bitcast.18, f32[3,2,2048]{2,1,0:T(2,128)S(1)} %bitcast.23), custom_call_target="tpu_custom_call" | custom-call | flops 10000000000 | bytes 8486912 | tf_op jit(solution)/shard_map/weights/pallas_call | solution.py:407
  73.0 1.3 %copy-done.8 = bf16[2,256,2048]{2,1,0:T(8,128)(2,1)} copy-done((bf16[2,256,2048]{2,1,0:T(8,128)(2,1)}, bf16[2,256,2048]{2,1,0:T(8,128)(2,1)S(1)}, u32[]{:S(2)}) %copy-start.8) | copy-done | bytes 2097176
  74.4 1.3 %copy-done.10 = bf16[2,256,2048]{2,1,0:T(8,128)(2,1)} copy-done((bf16[2,256,2048]{2,1,0:T(8,128)(2,1)}, bf16[2,256,2048]{2,1,0:T(8,128)(2,1)S(1)}, u32[]{:S(2)}) %copy-start.10) | copy-done | bytes 2097176
  75.7 1.3 %copy-done.12 = bf16[2,256,2048]{2,1,0:T(8,128)(2,1)} copy-done((bf16[2,256,2048]{2,1,0:T(8,128)(2,1)}, bf16[2,256,2048]{2,1,0:T(8,128)(2,1)S(1)}, u32[]{:S(2)}) %copy-start.12) | copy-done | bytes 2097176
  77.0 1.4 %copy-done.14 = bf16[2,256,2048]{2,1,0:T(8,128)(2,1)} copy-done((bf16[2,256,2048]{2,1,0:T(8,128)(2,1)}, bf16[2,256,2048]{2,1,0:T(8,128)(2,1)S(1)}, u32[]{:S(2)}) %copy-start.14) | copy-done | bytes 2097176
  78.4 8.5 %all-to-all-done.2 = f32[128,16,128]{2,1,0:T(8,128)S(1)} async-done(((f32[128,16,128]{2,1,0:T(8,128)}), f32[128,16,128]{2,1,0:T(8,128)S(1)}, u32[]{:S(2)}, u32[]{:S(2)}) %all-to-all-start.2) | async-done | bytes 1048608 | tf_op jit(solution)/shard_map/all_to_all | solution.py:432
  86.9 1.3 %inverse_z.1 = (bf16[2,512,256]{2,1,0:T(8,128)(2,1)S(1)}, bf16[2,512,256]{2,1,0:T(8,128)(2,1)S(1)}, f32[4,80,128]{2,1,0:T(8,128)S(1)}, f32[4,160,128]{2,1,0:T(8,128)S(1)}, f32[4,40,128]{2,1,0:T(8,128)S(1)}) custom-call(f32[2048,128]{1,0:T(8,128)S(1)} %bitcast.11, bf16[4,256,256]{2,1,0:T(8,128)(2,1)S(1)} %copy-done.6), custom_call_target="tpu_custom_call" | custom-call | flops 3000000000 | bytes 3194880 | tf_op jit(solution)/shard_map/inverse_z/pallas_call | solution.py:407
  88.3 0.9 collective-permute-start.3
  89.4 0.4 copy-done.13
  89.7 0.6 copy-done.15
  90.3 8.2 %gather.1.inner_ref = f32[3,2,2048]{2,1,0:T(2,128)S(1)} custom-call(s32[3,2,2048]{2,1,0:T(2,128)S(1)} %bitcast.19, f32[3,2,2048]{2,1,0:T(2,128)S(1)} %bitcast.24, bf16[2,256,2048]{2,1,0:T(8,128)(2,1)S(1)} %copy-done.9, bf16[2,256,2048]{2,1,0:T(8,128)(2,1)S(1)} %copy-done.11, bf16[2,256,2048]{2,1,0:T(8,128)(2,1)S(1)} %copy-done.13, ...), custom_call_target="tpu_custom_call" | custom-call | flops 12000000000 | bytes 9584640 | tf_op jit(solution)/shard_map/gather/pallas_call | solution.py:407
  98.6 2.7 %collective-permute-done.4.yr_ref = f32[4,160,128]{2,1,0:T(8,128)S(1)} collective-permute-done((f32[4,160,128]{2,1,0:T(8,128)S(1)}, f32[4,160,128]{2,1,0:T(8,128)S(1)}, u32[]{:S(2)}, u32[]{:S(2)}) %collective-permute-start.4) | collective-permute-done | bytes 327712 | tf_op jit(solution)/shard_map/ppermute | solution.py:428
  101.3 6.7 %gather_rim.1 = f32[3,2,2048]{2,1,0:T(2,128)} custom-call(s32[1,2]{1,0:T(1,128)S(1)} %bitcast.28, s32[3,2,2048]{2,1,0:T(2,128)S(1)} %bitcast.20, f32[3,2,2048]{2,1,0:T(2,128)S(1)} %bitcast.25, f32[2,2048]{1,0:T(2,128)S(1)} %copy-done.3, bf16[2,256,2048]{2,1,0:T(8,128)(2,1)S(1)} %copy-done.9, bf16[2,256,2048]{2,1,0:T(8,128)(2,1)S(1)} %copy-done.11, ...), custom_call_target="tpu_custom_call" | custom-call | flops 8000000000 | bytes 9175048 | tf_op jit(solution)/shard_map/gather_rim/pallas_call | solution.py:407
  (34 shorter events, 0.5 us)
Async XLA Ops:
  0.0 8.4 %copy-start.4 = (s32[2,1]{0,1:T(1,128)S(1)}, s32[2,1]{0,1:T(1,128)}, u32[]{:S(2)}) copy-start(s32[2,1]{0,1:T(1,128)} %param.11) | copy-start | bytes 28
  0.0 1.1 copy-start
  1.1 7.4 %copy-start.1 = (s32[2,3,2048]{2,0,1:T(2,128)S(1)}, s32[2,3,2048]{2,0,1:T(2,128)}, u32[]{:S(2)}) copy-start(s32[2,3,2048]{2,0,1:T(2,128)} %param.8) | copy-start | bytes 147460
  1.1 7.4 %copy-start.2 = (f32[2,3,2048]{2,0,1:T(2,128)S(1)}, f32[2,3,2048]{2,0,1:T(2,128)}, u32[]{:S(2)}) copy-start(f32[2,3,2048]{2,0,1:T(2,128)} %param.9) | copy-start | bytes 147460
  1.1 7.4 %copy-start.3 = (f32[2,2048]{1,0:T(2,128)S(1)}, f32[2,2048]{1,0:T(2,128)}, u32[]{:S(2)}) copy-start(f32[2,2048]{1,0:T(2,128)} %charge_ref.3) | copy-start | bytes 49156
  2.1 27.7 %all-to-all-start.1 = ((f32[8,64,256]{2,1,0:T(8,128)}), f32[8,64,256]{2,1,0:T(8,128)S(1)}, u32[]{:S(2)}, u32[]{:S(2)}) async-start(f32[8,64,256]{2,1,0:T(8,128)} %bitcast.6), calls=%async_computation.1 | async-start | bytes 1048576 | tf_op jit(solution)/shard_map/all_to_all | solution.py:465
  14.3 13.8 %collective-permute-start.2 = (f32[4,40,128]{2,1,0:T(8,128)S(1)}, f32[4,40,128]{2,1,0:T(8,128)S(1)}, u32[]{:S(2)}, u32[]{:S(2)}) collective-permute-start(f32[4,40,128]{2,1,0:T(8,128)S(1)} %get-tuple-element.27), channel_id=1, source_target_pairs={{0,127},{1,112},{2,113},{3,114},{4,115},{5,116},{6,117},{7,118},{8... | collective-permute-start | bytes 245768 | tf_op jit(solution)/shard_map/ppermute | solution.py:428
  21.1 7.0 %collective-permute-start = (f32[4,80,128]{2,1,0:T(8,128)S(1)}, f32[4,80,128]{2,1,0:T(8,128)S(1)}, u32[]{:S(2)}, u32[]{:S(2)}) collective-permute-start(f32[4,80,128]{2,1,0:T(8,128)S(1)} %get-tuple-element.25), channel_id=1, source_target_pairs={{0,112},{1,113},{2,114},{3,115},{4,116},{5,117},{6,118},{7,119},{8... | collective-permute-start | bytes 491528 | tf_op jit(solution)/shard_map/ppermute | solution.py:428
  21.1 7.2 %collective-permute-start.1 = (f32[4,160,128]{2,1,0:T(8,128)S(1)}, f32[4,160,128]{2,1,0:T(8,128)S(1)}, u32[]{:S(2)}, u32[]{:S(2)}) collective-permute-start(f32[4,160,128]{2,1,0:T(8,128)S(1)} %get-tuple-element.26), channel_id=1, source_target_pairs={{0,15},{1,0},{2,1},{3,2},{4,3},{5,4},{6,5},{7,6},{8,7},{9,8},{10,9... | collective-permute-start | bytes 983048 | tf_op jit(solution)/shard_map/ppermute | solution.py:428
  23.7 4.6 %copy-start.6 = (bf16[4,256,256]{2,1,0:T(8,128)(2,1)S(1)}, bf16[4,256,256]{2,1,0:T(8,128)(2,1)}, u32[]{:S(2)}) copy-start(bf16[4,256,256]{2,1,0:T(8,128)(2,1)} %constant.6.clone.zc) | copy-start | bytes 1572868
  28.3 28.5 %copy-start.7 = (bf16[4,256,256]{2,1,0:T(8,128)(2,1)S(1)}, bf16[4,256,256]{2,1,0:T(8,128)(2,1)}, u32[]{:S(2)}) copy-start(bf16[4,256,256]{2,1,0:T(8,128)(2,1)} %constant.7.clone.xc) | copy-start | bytes 1572868
  29.8 27.0 %copy-start.5 = (bf16[4,512,512]{2,1,0:T(8,128)(2,1)S(1)}, bf16[4,512,512]{2,1,0:T(8,128)(2,1)}, u32[]{:S(2)}) copy-start(bf16[4,512,512]{2,1,0:T(8,128)(2,1)} %constant.8.clone.yc) | copy-start | bytes 6291460
  63.3 23.6 %all-to-all-start.2 = ((f32[128,16,128]{2,1,0:T(8,128)}), f32[128,16,128]{2,1,0:T(8,128)S(1)}, u32[]{:S(2)}, u32[]{:S(2)}) async-start(f32[128,16,128]{2,1,0:T(8,128)} %bitcast.8), calls=%async_computation.2 | async-start | bytes 2097152 | tf_op jit(solution)/shard_map/all_to_all | solution.py:432
  73.0 1.3 %copy-start.8 = (bf16[2,256,2048]{2,1,0:T(8,128)(2,1)}, bf16[2,256,2048]{2,1,0:T(8,128)(2,1)S(1)}, u32[]{:S(2)}) copy-start(bf16[2,256,2048]{2,1,0:T(8,128)(2,1)S(1)} %get-tuple-element.19.wh_ref) | copy-start | bytes 6291460
  74.4 1.3 %copy-start.10 = (bf16[2,256,2048]{2,1,0:T(8,128)(2,1)}, bf16[2,256,2048]{2,1,0:T(8,128)(2,1)S(1)}, u32[]{:S(2)}) copy-start(bf16[2,256,2048]{2,1,0:T(8,128)(2,1)S(1)} %get-tuple-element.20.wl_ref) | copy-start | bytes 6291460
  75.7 1.4 %copy-start.12 = (bf16[2,256,2048]{2,1,0:T(8,128)(2,1)}, bf16[2,256,2048]{2,1,0:T(8,128)(2,1)S(1)}, u32[]{:S(2)}) copy-start(bf16[2,256,2048]{2,1,0:T(8,128)(2,1)S(1)} %get-tuple-element.21.sh_ref) | copy-start | bytes 6291460
  77.0 1.4 %copy-start.14 = (bf16[2,256,2048]{2,1,0:T(8,128)(2,1)}, bf16[2,256,2048]{2,1,0:T(8,128)(2,1)S(1)}, u32[]{:S(2)}) copy-start(bf16[2,256,2048]{2,1,0:T(8,128)(2,1)S(1)} %get-tuple-element.22.sl_ref) | copy-start | bytes 6291460
  86.9 2.5 %copy-start.9 = (bf16[2,256,2048]{2,1,0:T(8,128)(2,1)S(1)}, bf16[2,256,2048]{2,1,0:T(8,128)(2,1)}, u32[]{:S(2)}) copy-start(bf16[2,256,2048]{2,1,0:T(8,128)(2,1)} %copy-done.8) | copy-start | bytes 6291460
  86.9 2.5 %copy-start.11 = (bf16[2,256,2048]{2,1,0:T(8,128)(2,1)S(1)}, bf16[2,256,2048]{2,1,0:T(8,128)(2,1)}, u32[]{:S(2)}) copy-start(bf16[2,256,2048]{2,1,0:T(8,128)(2,1)} %copy-done.10) | copy-start | bytes 6291460
  86.9 2.9 %copy-start.13 = (bf16[2,256,2048]{2,1,0:T(8,128)(2,1)S(1)}, bf16[2,256,2048]{2,1,0:T(8,128)(2,1)}, u32[]{:S(2)}) copy-start(bf16[2,256,2048]{2,1,0:T(8,128)(2,1)} %copy-done.12) | copy-start | bytes 6291460
  86.9 3.5 %copy-start.15 = (bf16[2,256,2048]{2,1,0:T(8,128)(2,1)S(1)}, bf16[2,256,2048]{2,1,0:T(8,128)(2,1)}, u32[]{:S(2)}) copy-start(bf16[2,256,2048]{2,1,0:T(8,128)(2,1)} %copy-done.14) | copy-start | bytes 6291460
  88.2 10.4 %collective-permute-start.5 = (f32[4,40,128]{2,1,0:T(8,128)S(1)}, f32[4,40,128]{2,1,0:T(8,128)S(1)}, u32[]{:S(2)}, u32[]{:S(2)}) collective-permute-start(f32[4,40,128]{2,1,0:T(8,128)S(1)} %get-tuple-element.30), channel_id=1, source_target_pairs={{0,17},{1,18},{2,19},{3,20},{4,21},{5,22},{6,23},{7,24},{8,25},{9,... | collective-permute-start | bytes 245768 | tf_op jit(solution)/shard_map/ppermute | solution.py:428
  88.3 10.3 %collective-permute-start.3 = (f32[4,80,128]{2,1,0:T(8,128)S(1)}, f32[4,80,128]{2,1,0:T(8,128)S(1)}, u32[]{:S(2)}, u32[]{:S(2)}) collective-permute-start(f32[4,80,128]{2,1,0:T(8,128)S(1)} %get-tuple-element.28), channel_id=1, source_target_pairs={{0,16},{1,17},{2,18},{3,19},{4,20},{5,21},{6,22},{7,23},{8,24},{9,... | collective-permute-start | bytes 491528 | tf_op jit(solution)/shard_map/ppermute | solution.py:428
  89.1 12.1 %collective-permute-start.4 = (f32[4,160,128]{2,1,0:T(8,128)S(1)}, f32[4,160,128]{2,1,0:T(8,128)S(1)}, u32[]{:S(2)}, u32[]{:S(2)}) collective-permute-start(f32[4,160,128]{2,1,0:T(8,128)S(1)} %get-tuple-element.29), channel_id=1, source_target_pairs={{0,1},{1,2},{2,3},{3,4},{4,5},{5,6},{6,7},{7,8},{8,9},{9,10},{10,1... | collective-permute-start | bytes 983048 | tf_op jit(solution)/shard_map/ppermute | solution.py:428

commit v2 on v1

--- a/solution.py
+++ b/solution.py
@@ -17,7 +17,7 @@
 COLS = 16
 DEV = ROWS * COLS
 ATOMS = 2048
-CHUNK = 256
+CHUNK = 512
 RIM = 5
 INNER = XB * YB
 XRIM = RIM * YB
@@ -110,6 +110,27 @@
     return results
 
 
+def place_tables(cell, values, outs):
+    count = cell.shape[1]
+    base = (cell - lax.broadcasted_iota(jnp.int32, (16, count), 0)).astype(jnp.int16)
+    parts = []
+    for value in values:
+        rows = [split(jnp.broadcast_to(value[j], (16, count))) for j in range(6)]
+        parts.append(([row[0] for row in rows], [row[1] for row in rows]))
+    for g in range(K // 16):
+        behind = (base - jnp.int16(16 * g)) & jnp.int16(K - 1)
+        results = [[jnp.zeros((16, count), BF16)] * 2 for _ in values]
+        for j in range(6):
+            mask = behind == jnp.int16(j)
+            results = [
+                [jnp.where(mask, part[n][j], result[n]) for n in range(2)]
+                for part, result in zip(parts, results)
+            ]
+        for result, out in zip(results, outs):
+            for n in range(2):
+                out[n][g * 16 : g * 16 + 16, :] = result[n]
+
+
 def atom_rows(frac_ref, lanes):
     fraction = jnp.concatenate([frac_ref[d, :, lanes] for d in range(3)], axis=0)
     return spline_values(fraction)
@@ -149,8 +170,8 @@
 
 
 def spread_rim_kernel(
-    count_ref, cell_hbm, frac_hbm, charge_hbm, xr_ref, yr_ref, cr_ref, wh_ref, wl_ref,
-    cell_ref, frac_ref, charge_ref, ph, pq, sems,
+    count_ref, cell_hbm, frac_hbm, charge_hbm, xr_ref, yr_ref, cr_ref,
+    cell_ref, frac_ref, charge_ref, ph, pq, wh_ref, wl_ref, sems,
 ):
     copies = [
         pltpu.make_async_copy(source, target, sems.at[n])
@@ -165,8 +186,7 @@
     levels, _ = atom_rows(frac_ref, ALL)
     for s in range(2):
         (first,), (second,) = plane_rows(cell_ref, [levels], s, ALL)
-        (third,) = placed_rows(cell_ref[2, s : s + 1, :], [pick(levels, 2, s)], 0, K, True)
-        wh_ref[s], wl_ref[s] = split(third)
+        place_tables(cell_ref[2, s : s + 1, :], [pick(levels, 2, s)], [(wh_ref.at[s], wl_ref.at[s])])
         second = second * live_charges(charge_ref, count_ref, s, 0, ALL)
         p, q = ph.at[s], pq.at[s]
         for x in range(RIM):
@@ -181,11 +201,12 @@
         give(total, s, ((xr_ref, 0, XRIM), (yr_ref, XRIM, YRIM), (cr_ref, XRIM + YRIM, CRIM)))
 
 
-def spread_kernel(count_ref, cell_ref, frac_ref, charge_ref, wh_ref, wl_ref, mesh_ref, ph, pq):
+def spread_kernel(count_ref, cell_ref, frac_ref, charge_ref, mesh_ref, ph, pq, wh_ref, wl_ref):
     levels, _ = atom_rows(frac_ref, ALL)
     for s in range(2):
         (first,), (second,) = plane_rows(cell_ref, [levels], s, ALL)
         second = second * live_charges(charge_ref, count_ref, s, 0, ALL)
+        place_tables(cell_ref[2, s : s + 1, :], [pick(levels, 2, s)], [(wh_ref.at[s], wl_ref.at[s])])
         p, q = ph.at[s], pq.at[s]
         for y in range(YB):
             put(p, q, y * XB, second[8 + y : 9 + y] * first[8:])
@@ -196,11 +217,11 @@
 def weight_kernel(cell_ref, frac_ref, wh_ref, wl_ref, sh_ref, sl_ref):
     levels, slopes = atom_rows(frac_ref, ALL)
     for s in range(2):
-        value, slope = placed_rows(
-            cell_ref[2, s : s + 1, :], [pick(levels, 2, s), pick(slopes, 2, s)], 0, K, True
+        place_tables(
+            cell_ref[2, s : s + 1, :],
+            [pick(levels, 2, s), pick(slopes, 2, s)],
+            [(wh_ref.at[s], wl_ref.at[s]), (sh_ref.at[s], sl_ref.at[s])],
         )
-        wh_ref[s], wl_ref[s] = split(value)
-        sh_ref[s], sl_ref[s] = split(slope)
 
 
 def forward_z_kernel(mesh_ref, xr_ref, yr_ref, cr_ref, zc, out_ref, m):
@@ -247,7 +268,8 @@
 
 def plane_kernel(buf_ref, green_ref, yc, xc, out_ref, d, o):
     cosines, sines = (xc[0], xc[1]), (xc[2], xc[3])
-    for p in range(2):
+    planes = range(2)
+    for p in planes:
         for c in range(COLS):
             for g in range(2):
                 tiles = []
@@ -256,25 +278,36 @@
                     tiles.append(buf_ref[at : at + 8, :])
                 for low, tile in enumerate(exchange_blocks(tiles)):
                     at = (c * 4 + low) * 8
-                    d[at : at + 8, g * 128 : g * 128 + 128] = tile
-        first = dot3((yc[0], yc[1]), split(d[...]))
-        real, imag = split(first[:K]), split(first[K:])
-        f_real = dot3(real, cosines) + dot3(imag, sines)
-        f_imag = dot3(imag, cosines) - dot3(real, sines)
+                    d[p, at : at + 8, g * 128 : g * 128 + 128] = tile
+    first = [dot3((yc[0], yc[1]), split(d[p])) for p in planes]
+    parts = [(split(f[:K]), split(f[K:])) for f in first]
+    parts = [
+        (dot3(real, cosines) + dot3(imag, sines), dot3(imag, cosines) - dot3(real, sines))
+        for real, imag in parts
+    ]
+    scaled = []
+    for p in planes:
         green = jnp.concatenate(
             [green_ref[(r * 2 + p) * XB : (r * 2 + p + 1) * XB, :] for r in range(ROWS)], axis=0
         ) * (1.0 / float(K) ** 3)
-        real, imag = split(f_real * green), split(f_imag * green)
-        t_real = split(dot3(real, cosines) - dot3(imag, sines))
-        t_imag = split(dot3(imag, cosines) + dot3(real, sines))
-        both = tuple(jnp.concatenate([a, b], axis=0) for a, b in zip(t_real, t_imag))
-        o[...] = dot3((yc[2], yc[3]), both)
+        scaled.append([split(part * green) for part in parts[p]])
+    parts = [
+        (
+            split(dot3(real, cosines) - dot3(imag, sines)),
+            split(dot3(imag, cosines) + dot3(real, sines)),
+        )
+        for real, imag in scaled
+    ]
+    for p in planes:
+        both = tuple(jnp.concatenate([a, b], axis=0) for a, b in zip(*parts[p]))
+        o[p] = dot3((yc[2], yc[3]), both)
+    for p in planes:
         for c in range(COLS):
             for g in range(2):
                 tiles = []
                 for low in range(4):
                     at = (c * 4 + low) * 8
-                    tiles.append(o[at : at + 8, g * 128 : g * 128 + 128])
+                    tiles.append(o[p, at : at + 8, g * 128 : g * 128 + 128])
                 for r, tile in enumerate(exchange_blocks(tiles)):
                     at = ((g * 4 + r) * COLS + c) * 16 + p * 8
                     out_ref[at : at + 8, :] = tile
@@ -445,30 +478,34 @@
     rim_shapes = [shape(4, XRIM, 128), shape(4, YRIM, 128), shape(4, CRIM, 128)]
     weights = shape(2, K, ATOMS, dtype=BF16)
 
-    xr, yr, cr, wh, wl = call(
-        spread_rim_kernel, "spread_rim", 6e9, rim_shapes + [weights] * 2, atoms,
-        smem=(0,), hbm=(1, 2, 3),
+    table = pltpu.VMEM((2, K, ATOMS), BF16)
+    xr, yr, cr = call(
+        spread_rim_kernel, "spread_rim", 6e9, rim_shapes, atoms,
+        smem=(0,), hbm=(1, 2, 3), limit=60,
         scratch=[
             pltpu.VMEM((3, 2, ATOMS), jnp.int32),
             pltpu.VMEM((3, 2, ATOMS), F32),
             pltpu.VMEM((2, ATOMS), F32),
             pltpu.VMEM((2, RIMS + 8, ATOMS), BF16),
             pltpu.VMEM((2, RIMS + 8, ATOMS), BF16),
+            table,
+            table,
             pltpu.SemaphoreType.DMA((3,)),
         ],
     )
+    later, _ = lax.optimization_barrier((influence, cr))
     xr, yr, cr = shift(xr, -1, 0), shift(yr, 0, -1), shift(cr, -1, -1)
     green = call(
-        green_kernel, "green", 1e8, shape(512, K), (influence.reshape(XB * COLS, K),),
+        green_kernel, "green", 1e8, shape(512, K), (later.reshape(XB * COLS, K),),
         scratch=[pltpu.VMEM((512, 128), F32)],
     )
     green = lax.all_to_all(
         green.reshape(ROWS, 64, K), "row", split_axis=0, concat_axis=0, tiled=True
     ).reshape(512, K)
     mesh = call(
-        spread_kernel, "spread", 8e9, shape(4, INNER, 128), atoms + (wh, wl),
-        smem=(0,),
-        scratch=[pltpu.VMEM((2, INNER, ATOMS), BF16)] * 2,
+        spread_kernel, "spread", 8e9, shape(4, INNER, 128), atoms,
+        smem=(0,), limit=32,
+        scratch=[pltpu.VMEM((2, INNER, ATOMS), BF16)] * 2 + [table] * 2,
     )
     packed = call(
         forward_z_kernel, "forward_z", 3e9, shape(DEV * 16, 128), (mesh, xr, yr, cr, zc),
@@ -478,7 +515,7 @@
     wh, wl, gh, gl = call(weight_kernel, "weights", 1e10, [weights] * 4, (cells, fractions))
     packed = call(
         plane_kernel, "planes", 6e9, shape(DEV * 16, 128), (packed, green, yc, xc),
-        scratch=[pltpu.VMEM((512, K), F32)] * 2,
+        scratch=[pltpu.VMEM((2, 512, K), F32)] * 2,
     )
     packed = everywhere(packed.reshape(DEV, 16, 128)).reshape(DEV * 16, 128)
     fh, fl, xr, yr, cr = call(

time: 108 us -> 105 us (0.972)
  waiting for transfers between devices: 11.3 us -> 13.9 us
  blocking collectives: 27 us -> 24.9 us
  starting transfers between devices: 21.5 us -> 19.9 us
  Pallas kernels: 40.5 us -> 39.3 us
    all_to_all x1, starting transfers between devices: 6.35 us -> 3.49 us  [shards(): lax.all_to_all(green.reshape(ROWS, 64, K), 'row', split_axis=0, concat_ax...]
    all_to_all x1, blocking collectives: 27 us -> 24.9 us  [everywhere(): lax.all_to_all(value, ('row', 'col'), split_axis=0, concat_axis=0, tiled=...]
    all_to_all x1, waiting for transfers between devices: 0.01 us -> 1.65 us  [shards(): lax.all_to_all(green.reshape(ROWS, 64, K), 'row', split_axis=0, concat_ax...]
    ppermute x6, starting transfers between devices: 10.6 us -> 11.8 us  [shift(): return lax.ppermute(value, ('row', 'col'), pairs)]
    pallas_call x9, Pallas kernels: 40.5 us -> 39.3 us  [call(): pl.pallas_call(kernel, out_shape=out_shape, in_specs=[spec(n) for n in ra...]
  transfers between devices with their start and end apart: 8 -> 8, of which waited for: 3 -> 3; matrix products, arithmetic and copies ran while one was open for 0% -> 0% of each run, Pallas kernels for 23% -> 19%
where the time goes in v2:
time: 105 us
  Pallas kernels  39.3 us (37%)
  blocking collectives  24.9 us (24%)
  starting transfers between devices  19.9 us (19%)
  waiting for transfers between devices  13.9 us (13%)
  local copies, waits for them, and re-layouts  6.43 us (6%)
    pallas_call x9, Pallas kernels, call(): pl.pallas_call(kernel, out_shape=out_shape, in_specs=[spec(n) for n in ra...  39.3 us
    all_to_all x1, blocking collectives, everywhere(): lax.all_to_all(value, ('row', 'col'), split_axis=0, concat_axis=0, tiled=...  24.9 us
    ppermute x6, starting transfers between devices, shift(): return lax.ppermute(value, ('row', 'col'), pairs)  11.8 us
    all_to_all x1, waiting for transfers between devices, everywhere(): lax.all_to_all(value, ('row', 'col'), split_axis=0, concat_axis=0, tiled=...  9.42 us
    unnamed x32, local copies, waits for them, and re-layouts  6.43 us
    all_to_all x1, starting transfers between devices, everywhere(): lax.all_to_all(value, ('row', 'col'), split_axis=0, concat_axis=0, tiled=...  4.63 us
    all_to_all x1, starting transfers between devices, shards(): lax.all_to_all(green.reshape(ROWS, 64, K), 'row', split_axis=0, concat_ax...  3.49 us
    ppermute x6, waiting for transfers between devices, shift(): return lax.ppermute(value, ('row', 'col'), pairs)  2.86 us
  transfers between devices with their start and end apart: 8, of which 3 were waited for; matrix products, arithmetic and copies ran while one was open for 0% of the time, Pallas kernels for 19%

profile of v2, /device:TPU:0, one launch (start us, length us, event | category | flops | bytes accessed | tf_op | source)
XLA Modules:
  0.0 104.7 jit_solution(5361761913079500555)
XLA Ops:
  0.0 6.4 %spread_rim.1 = (f32[4,80,128]{2,1,0:T(8,128)}, f32[4,160,128]{2,1,0:T(8,128)}, f32[4,40,128]{2,1,0:T(8,128)}) custom-call(s32[1,2]{1,0:T(1,128)} %bitcast.26, s32[3,2,2048]{2,1,0:T(2,128)} %bitcast.16, f32[3,2,2048]{2,1,0:T(2,128)} %bitcast.21, f32[2,2048]{1,0:T(2,128)} %charge_ref.3), custom_call_target="tpu_custom_call" | custom-call | flops 6000000000 | bytes 688136 | tf_op jit(solution)/shard_map/spread_rim/pallas_call | solution.py:440
  6.5 8.3 %collective-permute-start.2 = (f32[4,40,128]{2,1,0:T(8,128)}, f32[4,40,128]{2,1,0:T(8,128)S(1)}, u32[]{:S(2)}, u32[]{:S(2)}) collective-permute-start(f32[4,40,128]{2,1,0:T(8,128)} %get-tuple-element.24), channel_id=1, source_target_pairs={{0,127},{1,112},{2,113},{3,114},{4,115},{5,116},{6,117},{7,118},{8... | collective-permute-start | bytes 245768 | tf_op jit(solution)/shard_map/ppermute | solution.py:461
  15.0 2.1 %collective-permute-start.1 = (f32[4,160,128]{2,1,0:T(8,128)}, f32[4,160,128]{2,1,0:T(8,128)S(1)}, u32[]{:S(2)}, u32[]{:S(2)}) collective-permute-start(f32[4,160,128]{2,1,0:T(8,128)} %get-tuple-element.23), channel_id=1, source_target_pairs={{0,15},{1,0},{2,1},{3,2},{4,3},{5,4},{6,5},{7,6},{8,7},{9,8},{10,9... | collective-permute-start | bytes 983048 | tf_op jit(solution)/shard_map/ppermute | solution.py:461
  17.1 1.0 green.1
  18.1 3.5 %all-to-all-start.1 = ((f32[8,64,256]{2,1,0:T(8,128)}), f32[8,64,256]{2,1,0:T(8,128)S(1)}, u32[]{:S(2)}, u32[]{:S(2)}) async-start(f32[8,64,256]{2,1,0:T(8,128)} %bitcast.6), calls=%async_computation.1 | async-start | bytes 1048576 | tf_op jit(solution)/shard_map/all_to_all | solution.py:502
  21.6 5.7 %spread.1.mesh_ref = f32[4,512,128]{2,1,0:T(8,128)S(1)} custom-call(s32[1,2]{1,0:T(1,128)S(1)} %bitcast.27, s32[3,2,2048]{2,1,0:T(2,128)S(1)} %bitcast.17, f32[3,2,2048]{2,1,0:T(2,128)S(1)} %bitcast.22, f32[2,2048]{1,0:T(2,128)S(1)} %copy-done.3), custom_call_target="tpu_custom_call" | custom-call | flops 8000000000 | bytes 1163272 | tf_op jit(solution)/shard_map/spread/pallas_call | solution.py:440
  27.4 1.5 %forward_z.1 = f32[2048,128]{1,0:T(8,128)S(1)} custom-call(f32[4,512,128]{2,1,0:T(8,128)S(1)} %spread.1.mesh_ref, f32[4,80,128]{2,1,0:T(8,128)S(1)} %collective-permute-done.xr_ref, f32[4,160,128]{2,1,0:T(8,128)S(1)} %collective-permute-done.1.yr_ref, f32[4,40,128]{2,1,0:T(8,128)S(1)} %collective-permute-done.2.cr_ref, bf16[4,256,256]{2,1,0:T(8,128)(2,1)S(1)} %copy-done.6), custom_call_target="tpu_custom_call" | custom-call | flops 3000000000 | bytes 3194880 | tf_op jit(solution)/shard_map/forward_z/pallas_call | solution.py:440
  28.8 1.6 %all-to-all-done.1 = f32[8,64,256]{2,1,0:T(8,128)S(1)} async-done(((f32[8,64,256]{2,1,0:T(8,128)}), f32[8,64,256]{2,1,0:T(8,128)S(1)}, u32[]{:S(2)}, u32[]{:S(2)}) %all-to-all-start.1) | async-done | bytes 524320 | tf_op jit(solution)/shard_map/all_to_all | solution.py:502
  30.5 24.9 %all_to_all.15 = f32[128,16,128]{2,1,0:T(8,128)S(1)} all-to-all(f32[128,16,128]{2,1,0:T(8,128)S(1)} %bitcast.12), channel_id=1, replica_groups=mesh['row'=8,'col'=16] {'row','col'}, dimensions={0} | all-to-all | bytes 2097152 | tf_op jit(solution)/shard_map/all_to_all | solution.py:465
  55.4 5.2 %planes.1 = f32[2048,128]{1,0:T(8,128)} custom-call(f32[2048,128]{1,0:T(8,128)S(1)} %bitcast.13, f32[512,256]{1,0:T(8,128)S(1)} %bitcast.15, bf16[4,512,512]{2,1,0:T(8,128)(2,1)S(1)} %copy-done.5, bf16[4,256,256]{2,1,0:T(8,128)(2,1)S(1)} %copy-done.7), custom_call_target="tpu_custom_call" | custom-call | flops 6000000000 | bytes 5242880 | tf_op jit(solution)/shard_map/planes/pallas_call | solution.py:440
  60.7 4.6 %all-to-all-start.2 = ((f32[128,16,128]{2,1,0:T(8,128)}), f32[128,16,128]{2,1,0:T(8,128)S(1)}, u32[]{:S(2)}, u32[]{:S(2)}) async-start(f32[128,16,128]{2,1,0:T(8,128)} %bitcast.8), calls=%async_computation.2 | async-start | bytes 2097152 | tf_op jit(solution)/shard_map/all_to_all | solution.py:465
  65.3 4.1 %weights.1 = (bf16[2,256,2048]{2,1,0:T(8,128)(2,1)S(1)}, bf16[2,256,2048]{2,1,0:T(8,128)(2,1)S(1)}, bf16[2,256,2048]{2,1,0:T(8,128)(2,1)S(1)}, bf16[2,256,2048]{2,1,0:T(8,128)(2,1)S(1)}) custom-call(s32[3,2,2048]{2,1,0:T(2,128)S(1)} %bitcast.18, f32[3,2,2048]{2,1,0:T(2,128)S(1)} %bitcast.23), custom_call_target="tpu_custom_call" | custom-call | flops 10000000000 | bytes 8486912 | tf_op jit(solution)/shard_map/weights/pallas_call | solution.py:440
  69.4 1.3 %copy-done.8 = bf16[2,256,2048]{2,1,0:T(8,128)(2,1)} copy-done((bf16[2,256,2048]{2,1,0:T(8,128)(2,1)}, bf16[2,256,2048]{2,1,0:T(8,128)(2,1)S(1)}, u32[]{:S(2)}) %copy-start.8) | copy-done | bytes 2097176
  70.7 1.3 %copy-done.10 = bf16[2,256,2048]{2,1,0:T(8,128)(2,1)} copy-done((bf16[2,256,2048]{2,1,0:T(8,128)(2,1)}, bf16[2,256,2048]{2,1,0:T(8,128)(2,1)S(1)}, u32[]{:S(2)}) %copy-start.10) | copy-done | bytes 2097176
  72.1 1.3 %copy-done.12 = bf16[2,256,2048]{2,1,0:T(8,128)(2,1)} copy-done((bf16[2,256,2048]{2,1,0:T(8,128)(2,1)}, bf16[2,256,2048]{2,1,0:T(8,128)(2,1)S(1)}, u32[]{:S(2)}) %copy-start.12) | copy-done | bytes 2097176
  73.4 1.4 %copy-done.14 = bf16[2,256,2048]{2,1,0:T(8,128)(2,1)} copy-done((bf16[2,256,2048]{2,1,0:T(8,128)(2,1)}, bf16[2,256,2048]{2,1,0:T(8,128)(2,1)S(1)}, u32[]{:S(2)}) %copy-start.14) | copy-done | bytes 2097176
  74.8 9.4 %all-to-all-done.2 = f32[128,16,128]{2,1,0:T(8,128)S(1)} async-done(((f32[128,16,128]{2,1,0:T(8,128)}), f32[128,16,128]{2,1,0:T(8,128)S(1)}, u32[]{:S(2)}, u32[]{:S(2)}) %all-to-all-start.2) | async-done | bytes 1048608 | tf_op jit(solution)/shard_map/all_to_all | solution.py:465
  84.2 1.3 %inverse_z.1 = (bf16[2,512,256]{2,1,0:T(8,128)(2,1)S(1)}, bf16[2,512,256]{2,1,0:T(8,128)(2,1)S(1)}, f32[4,80,128]{2,1,0:T(8,128)S(1)}, f32[4,160,128]{2,1,0:T(8,128)S(1)}, f32[4,40,128]{2,1,0:T(8,128)S(1)}) custom-call(f32[2048,128]{1,0:T(8,128)S(1)} %bitcast.11, bf16[4,256,256]{2,1,0:T(8,128)(2,1)S(1)} %copy-done.6), custom_call_target="tpu_custom_call" | custom-call | flops 3000000000 | bytes 3194880 | tf_op jit(solution)/shard_map/inverse_z/pallas_call | solution.py:440
  85.6 0.9 collective-permute-start.3
  86.7 0.4 copy-done.13
  87.1 0.6 copy-done.15
  87.7 8.1 %gather.1.inner_ref = f32[3,2,2048]{2,1,0:T(2,128)S(1)} custom-call(s32[3,2,2048]{2,1,0:T(2,128)S(1)} %bitcast.19, f32[3,2,2048]{2,1,0:T(2,128)S(1)} %bitcast.24, bf16[2,256,2048]{2,1,0:T(8,128)(2,1)S(1)} %copy-done.9, bf16[2,256,2048]{2,1,0:T(8,128)(2,1)S(1)} %copy-done.11, bf16[2,256,2048]{2,1,0:T(8,128)(2,1)S(1)} %copy-done.13, ...), custom_call_target="tpu_custom_call" | custom-call | flops 12000000000 | bytes 9584640 | tf_op jit(solution)/shard_map/gather/pallas_call | solution.py:440
  95.8 2.8 %collective-permute-done.4.yr_ref = f32[4,160,128]{2,1,0:T(8,128)S(1)} collective-permute-done((f32[4,160,128]{2,1,0:T(8,128)S(1)}, f32[4,160,128]{2,1,0:T(8,128)S(1)}, u32[]{:S(2)}, u32[]{:S(2)}) %collective-permute-start.4) | collective-permute-done | bytes 327712 | tf_op jit(solution)/shard_map/ppermute | solution.py:461
  98.6 6.1 %gather_rim.1 = f32[3,2,2048]{2,1,0:T(2,128)} custom-call(s32[1,2]{1,0:T(1,128)S(1)} %bitcast.28, s32[3,2,2048]{2,1,0:T(2,128)S(1)} %bitcast.20, f32[3,2,2048]{2,1,0:T(2,128)S(1)} %bitcast.25, f32[2,2048]{1,0:T(2,128)S(1)} %copy-done.3, bf16[2,256,2048]{2,1,0:T(8,128)(2,1)S(1)} %copy-done.9, bf16[2,256,2048]{2,1,0:T(8,128)(2,1)S(1)} %copy-done.11, ...), custom_call_target="tpu_custom_call" | custom-call | flops 8000000000 | bytes 9175048 | tf_op jit(solution)/shard_map/gather_rim/pallas_call | solution.py:440
  (34 shorter events, 0.6 us)
Async XLA Ops:
  0.0 17.1 %copy-start = (f32[32,16,256]{2,1,0:T(8,128)S(1)}, f32[32,16,256]{2,1,0:T(8,128)}, u32[]{:S(2)}) copy-start(f32[32,16,256]{2,1,0:T(8,128)} %param.12) | copy-start | bytes 1572868
  6.4 15.2 %copy-start.1 = (s32[2,3,2048]{2,0,1:T(2,128)S(1)}, s32[2,3,2048]{2,0,1:T(2,128)}, u32[]{:S(2)}) copy-start(s32[2,3,2048]{2,0,1:T(2,128)} %param.8) | copy-start | bytes 147460
  6.4 15.2 %copy-start.2 = (f32[2,3,2048]{2,0,1:T(2,128)S(1)}, f32[2,3,2048]{2,0,1:T(2,128)}, u32[]{:S(2)}) copy-start(f32[2,3,2048]{2,0,1:T(2,128)} %param.9) | copy-start | bytes 147460
  6.4 15.2 %copy-start.3 = (f32[2,2048]{1,0:T(2,128)S(1)}, f32[2,2048]{1,0:T(2,128)}, u32[]{:S(2)}) copy-start(f32[2,2048]{1,0:T(2,128)} %charge_ref.3) | copy-start | bytes 49156
  6.4 15.2 %copy-start.4 = (s32[2,1]{0,1:T(1,128)S(1)}, s32[2,1]{0,1:T(1,128)}, u32[]{:S(2)}) copy-start(s32[2,1]{0,1:T(1,128)} %param.11) | copy-start | bytes 28
  6.5 20.8 %collective-permute-start.2 = (f32[4,40,128]{2,1,0:T(8,128)}, f32[4,40,128]{2,1,0:T(8,128)S(1)}, u32[]{:S(2)}, u32[]{:S(2)}) collective-permute-start(f32[4,40,128]{2,1,0:T(8,128)} %get-tuple-element.24), channel_id=1, source_target_pairs={{0,127},{1,112},{2,113},{3,114},{4,115},{5,116},{6,117},{7,118},{8... | collective-permute-start | bytes 245768 | tf_op jit(solution)/shard_map/ppermute | solution.py:461
  14.8 12.5 %collective-permute-start = (f32[4,80,128]{2,1,0:T(8,128)}, f32[4,80,128]{2,1,0:T(8,128)S(1)}, u32[]{:S(2)}, u32[]{:S(2)}) collective-permute-start(f32[4,80,128]{2,1,0:T(8,128)} %get-tuple-element.22), channel_id=1, source_target_pairs={{0,112},{1,113},{2,114},{3,115},{4,116},{5,117},{6,118},{7,119},{8... | collective-permute-start | bytes 491528 | tf_op jit(solution)/shard_map/ppermute | solution.py:461
  15.0 12.3 %collective-permute-start.1 = (f32[4,160,128]{2,1,0:T(8,128)}, f32[4,160,128]{2,1,0:T(8,128)S(1)}, u32[]{:S(2)}, u32[]{:S(2)}) collective-permute-start(f32[4,160,128]{2,1,0:T(8,128)} %get-tuple-element.23), channel_id=1, source_target_pairs={{0,15},{1,0},{2,1},{3,2},{4,3},{5,4},{6,5},{7,6},{8,7},{9,8},{10,9... | collective-permute-start | bytes 983048 | tf_op jit(solution)/shard_map/ppermute | solution.py:461
  18.1 12.4 %all-to-all-start.1 = ((f32[8,64,256]{2,1,0:T(8,128)}), f32[8,64,256]{2,1,0:T(8,128)S(1)}, u32[]{:S(2)}, u32[]{:S(2)}) async-start(f32[8,64,256]{2,1,0:T(8,128)} %bitcast.6), calls=%async_computation.1 | async-start | bytes 1048576 | tf_op jit(solution)/shard_map/all_to_all | solution.py:502
  21.6 5.7 %copy-start.6 = (bf16[4,256,256]{2,1,0:T(8,128)(2,1)S(1)}, bf16[4,256,256]{2,1,0:T(8,128)(2,1)}, u32[]{:S(2)}) copy-start(bf16[4,256,256]{2,1,0:T(8,128)(2,1)} %constant.6.clone.zc) | copy-start | bytes 1572868
  27.3 28.1 %copy-start.7 = (bf16[4,256,256]{2,1,0:T(8,128)(2,1)S(1)}, bf16[4,256,256]{2,1,0:T(8,128)(2,1)}, u32[]{:S(2)}) copy-start(bf16[4,256,256]{2,1,0:T(8,128)(2,1)} %constant.7.clone.xc) | copy-start | bytes 1572868
  30.5 24.9 %copy-start.5 = (bf16[4,512,512]{2,1,0:T(8,128)(2,1)S(1)}, bf16[4,512,512]{2,1,0:T(8,128)(2,1)}, u32[]{:S(2)}) copy-start(bf16[4,512,512]{2,1,0:T(8,128)(2,1)} %constant.8.clone.yc) | copy-start | bytes 6291460
  60.7 23.6 %all-to-all-start.2 = ((f32[128,16,128]{2,1,0:T(8,128)}), f32[128,16,128]{2,1,0:T(8,128)S(1)}, u32[]{:S(2)}, u32[]{:S(2)}) async-start(f32[128,16,128]{2,1,0:T(8,128)} %bitcast.8), calls=%async_computation.2 | async-start | bytes 2097152 | tf_op jit(solution)/shard_map/all_to_all | solution.py:465
  69.4 1.3 %copy-start.8 = (bf16[2,256,2048]{2,1,0:T(8,128)(2,1)}, bf16[2,256,2048]{2,1,0:T(8,128)(2,1)S(1)}, u32[]{:S(2)}) copy-start(bf16[2,256,2048]{2,1,0:T(8,128)(2,1)S(1)} %get-tuple-element.18.wh_ref) | copy-start | bytes 6291460
  70.7 1.3 %copy-start.10 = (bf16[2,256,2048]{2,1,0:T(8,128)(2,1)}, bf16[2,256,2048]{2,1,0:T(8,128)(2,1)S(1)}, u32[]{:S(2)}) copy-start(bf16[2,256,2048]{2,1,0:T(8,128)(2,1)S(1)} %get-tuple-element.19.wl_ref) | copy-start | bytes 6291460
  72.1 1.4 %copy-start.12 = (bf16[2,256,2048]{2,1,0:T(8,128)(2,1)}, bf16[2,256,2048]{2,1,0:T(8,128)(2,1)S(1)}, u32[]{:S(2)}) copy-start(bf16[2,256,2048]{2,1,0:T(8,128)(2,1)S(1)} %get-tuple-element.20.sh_ref) | copy-start | bytes 6291460
  73.4 1.4 %copy-start.14 = (bf16[2,256,2048]{2,1,0:T(8,128)(2,1)}, bf16[2,256,2048]{2,1,0:T(8,128)(2,1)S(1)}, u32[]{:S(2)}) copy-start(bf16[2,256,2048]{2,1,0:T(8,128)(2,1)S(1)} %get-tuple-element.21.sl_ref) | copy-start | bytes 6291460
  84.2 2.5 %copy-start.9 = (bf16[2,256,2048]{2,1,0:T(8,128)(2,1)S(1)}, bf16[2,256,2048]{2,1,0:T(8,128)(2,1)}, u32[]{:S(2)}) copy-start(bf16[2,256,2048]{2,1,0:T(8,128)(2,1)} %copy-done.8) | copy-start | bytes 6291460
  84.2 2.5 %copy-start.11 = (bf16[2,256,2048]{2,1,0:T(8,128)(2,1)S(1)}, bf16[2,256,2048]{2,1,0:T(8,128)(2,1)}, u32[]{:S(2)}) copy-start(bf16[2,256,2048]{2,1,0:T(8,128)(2,1)} %copy-done.10) | copy-start | bytes 6291460
  84.2 2.9 %copy-start.13 = (bf16[2,256,2048]{2,1,0:T(8,128)(2,1)S(1)}, bf16[2,256,2048]{2,1,0:T(8,128)(2,1)}, u32[]{:S(2)}) copy-start(bf16[2,256,2048]{2,1,0:T(8,128)(2,1)} %copy-done.12) | copy-start | bytes 6291460
  84.2 3.5 %copy-start.15 = (bf16[2,256,2048]{2,1,0:T(8,128)(2,1)S(1)}, bf16[2,256,2048]{2,1,0:T(8,128)(2,1)}, u32[]{:S(2)}) copy-start(bf16[2,256,2048]{2,1,0:T(8,128)(2,1)} %copy-done.14) | copy-start | bytes 6291460
  85.5 10.2 %collective-permute-start.5 = (f32[4,40,128]{2,1,0:T(8,128)S(1)}, f32[4,40,128]{2,1,0:T(8,128)S(1)}, u32[]{:S(2)}, u32[]{:S(2)}) collective-permute-start(f32[4,40,128]{2,1,0:T(8,128)S(1)} %get-tuple-element.28), channel_id=1, source_target_pairs={{0,17},{1,18},{2,19},{3,20},{4,21},{5,22},{6,23},{7,24},{8,25},{9,... | collective-permute-start | bytes 245768 | tf_op jit(solution)/shard_map/ppermute | solution.py:461
  85.6 10.2 %collective-permute-start.3 = (f32[4,80,128]{2,1,0:T(8,128)S(1)}, f32[4,80,128]{2,1,0:T(8,128)S(1)}, u32[]{:S(2)}, u32[]{:S(2)}) collective-permute-start(f32[4,80,128]{2,1,0:T(8,128)S(1)} %get-tuple-element.26), channel_id=1, source_target_pairs={{0,16},{1,17},{2,18},{3,19},{4,20},{5,21},{6,22},{7,23},{8,24},{9,... | collective-permute-start | bytes 491528 | tf_op jit(solution)/shard_map/ppermute | solution.py:461
  86.5 12.1 %collective-permute-start.4 = (f32[4,160,128]{2,1,0:T(8,128)S(1)}, f32[4,160,128]{2,1,0:T(8,128)S(1)}, u32[]{:S(2)}, u32[]{:S(2)}) collective-permute-start(f32[4,160,128]{2,1,0:T(8,128)S(1)} %get-tuple-element.27), channel_id=1, source_target_pairs={{0,1},{1,2},{2,3},{3,4},{4,5},{5,6},{6,7},{7,8},{8,9},{9,10},{10,1... | collective-permute-start | bytes 983048 | tf_op jit(solution)/shard_map/ppermute | solution.py:461

commit v3 on v2

--- a/solution.py
+++ b/solution.py
@@ -25,6 +25,7 @@
 CRIM = RIM * 8
 RIMS = XRIM + YRIM + CRIM
 VMEM_ALL = pl.BlockSpec(memory_space=pltpu.VMEM)
+HBM_ALL = pl.BlockSpec(memory_space=pltpu.HBM)
 SMEM_ALL = pl.BlockSpec(memory_space=pltpu.SMEM)
 
 
@@ -214,14 +215,32 @@
         give(total, s, ((mesh_ref, 0, INNER),))
 
 
-def weight_kernel(cell_ref, frac_ref, wh_ref, wl_ref, sh_ref, sl_ref):
-    levels, slopes = atom_rows(frac_ref, ALL)
+TALL, WIDE = XB + 8, YB + 8
+SIDES = 2 * TALL + 2 * WIDE
+
+
+def weight_kernel(count_ref, cell_ref, frac_ref, charge_ref, wh_ref, wl_ref, sh_ref, sl_ref, xy_ref):
+    tables = atom_rows(frac_ref, ALL)
     for s in range(2):
         place_tables(
             cell_ref[2, s : s + 1, :],
-            [pick(levels, 2, s), pick(slopes, 2, s)],
+            [pick(t, 2, s) for t in tables],
             [(wh_ref.at[s], wl_ref.at[s]), (sh_ref.at[s], sl_ref.at[s])],
         )
+        xs, ys = plane_rows(cell_ref, tables, s, ALL)
+        charges = -live_charges(charge_ref, count_ref, s, 0, ALL)
+        xy_ref[s, :TALL, :] = xs[0]
+        xy_ref[s, TALL : 2 * TALL, :] = xs[1]
+        xy_ref[s, 2 * TALL : 2 * TALL + WIDE, :] = ys[0] * charges
+        xy_ref[s, 2 * TALL + WIDE :, :] = ys[1] * charges
+
+
+def side_weights(xy_ref, s, lanes):
+    xy = xy_ref[s, :, lanes]
+    return (
+        (xy[:TALL], xy[TALL : 2 * TALL]),
+        (xy[2 * TALL : 2 * TALL + WIDE], xy[2 * TALL + WIDE :]),
+    )
 
 
 def forward_z_kernel(mesh_ref, xr_ref, yr_ref, cr_ref, zc, out_ref, m):
@@ -371,11 +390,10 @@
     lax.fori_loop(0, ATOMS // CHUNK, step, 0)
 
 
-def gather_kernel(cell_ref, frac_ref, wh_ref, wl_ref, sh_ref, sl_ref, fh_ref, fl_ref, out_ref):
+def gather_kernel(xy_ref, wh_ref, wl_ref, sh_ref, sl_ref, fh_ref, fl_ref, out_ref):
     def body(at, lanes):
-        tables = atom_rows(frac_ref, lanes)
         for s in range(2):
-            xs, ys = plane_rows(cell_ref, tables, s, lanes)
+            xs, ys = side_weights(xy_ref, s, lanes)
             field = fh_ref[s], fl_ref[s]
             plain = dot3(field, (wh_ref[s, :, lanes], wl_ref[s, :, lanes]))
             sloped = dot3(field, (sh_ref[s, :, lanes], sl_ref[s, :, lanes]))
@@ -388,8 +406,7 @@
 
 
 def gather_rim_kernel(
-    count_ref, cell_ref, frac_ref, charge_ref, wh_ref, wl_ref, sh_ref, sl_ref,
-    xr_ref, yr_ref, cr_ref, inner_ref, out_ref, fh, fl,
+    xy_ref, wh_ref, wl_ref, sh_ref, sl_ref, xr_ref, yr_ref, cr_ref, inner_ref, out_ref, fh, fl,
 ):
     for s in range(2):
         for h in range(2):
@@ -401,9 +418,8 @@
                 fl[s, at : at + value.shape[0], columns] = rest
 
     def body(at, lanes):
-        tables = atom_rows(frac_ref, lanes)
         for s in range(2):
-            xs, ys = plane_rows(cell_ref, tables, s, lanes)
+            xs, ys = side_weights(xy_ref, s, lanes)
             field = fh[s], fl[s]
             plain = dot3(field, (wh_ref[s, :, lanes], wl_ref[s, :, lanes]))
             sloped = dot3(field, (sh_ref[s, :, lanes], sl_ref[s, :, lanes]))
@@ -412,10 +428,9 @@
             side = weighed(plain, sloped, 0, columns, (ys[0][8:], ys[1][8:]))
             edge = weighed(plain, sloped, XRIM, lines, (xs[0][8:], xs[1][8:]))
             corner = weighed(plain, sloped, XRIM + YRIM, lines, (xs[0][:8], xs[1][:8]))
-            charges = live_charges(charge_ref, count_ref, s, at, lanes)
             for d, e in ((0, 1), (1, 0), (2, 2)):
                 force = inner_ref[d, s : s + 1, lanes] + side[e] + edge[d] + corner[d]
-                out_ref[d, s : s + 1, lanes] = -charges * force
+                out_ref[d, s : s + 1, lanes] = force
 
     chunks(body)
 
@@ -431,7 +446,7 @@
 def call(kernel, name, flops, out_shape, operands, smem=(), hbm=(), scratch=(), limit=24):
     def spec(n):
         if n in hbm:
-            return pl.BlockSpec(memory_space=pltpu.HBM)
+            return HBM_ALL
         return SMEM_ALL if n in smem else VMEM_ALL
 
     single = not isinstance(out_shape, list)
@@ -512,7 +527,9 @@
         scratch=[pltpu.VMEM((4, INNER, 128), F32)],
     )
     packed = everywhere(packed.reshape(DEV, 16, 128)).reshape(DEV * 16, 128)
-    wh, wl, gh, gl = call(weight_kernel, "weights", 1e10, [weights] * 4, (cells, fractions))
+    wh, wl, gh, gl, xy = call(
+        weight_kernel, "weights", 1e10, [weights] * 4 + [shape(2, SIDES, ATOMS)], atoms, smem=(0,)
+    )
     packed = call(
         plane_kernel, "planes", 6e9, shape(DEV * 16, 128), (packed, green, yc, xc),
         scratch=[pltpu.VMEM((2, 512, K), F32)] * 2,
@@ -526,11 +543,11 @@
     xr, yr, cr = shift(xr, 1, 0), shift(yr, 0, 1), shift(cr, 1, 1)
     inner = call(
         gather_kernel, "gather", 1.2e10, shape(3, 2, ATOMS),
-        (cells, fractions, wh, wl, gh, gl, fh, fl),
+        (xy, wh, wl, gh, gl, fh, fl),
     )
     forces = call(
         gather_rim_kernel, "gather_rim", 8e9, shape(3, 2, ATOMS),
-        atoms + (wh, wl, gh, gl, xr, yr, cr, inner), smem=(0,),
+        (xy, wh, wl, gh, gl, xr, yr, cr, inner),
         scratch=[pltpu.VMEM((2, RIMS + 8, K), BF16)] * 2,
     )
     return jnp.transpose(forces, (1, 0, 2))

time: 105 us -> 104 us (level)
  waiting for transfers between devices: 13.9 us -> 11 us
  local copies, waits for them, and re-layouts: 6.43 us -> 8.39 us
    all_to_all x1, waiting for transfers between devices: 9.42 us -> 6.38 us  [everywhere(): lax.all_to_all(value, ('row', 'col'), split_axis=0, concat_axis=0, tiled=...]
    unnamed x32 -> x36, local copies, waits for them, and re-layouts: 6.43 us -> 8.39 us
  transfers between devices with their start and end apart: 8 -> 8, of which waited for: 3 -> 5; matrix products, arithmetic and copies ran while one was open for 0% -> 0% of each run, Pallas kernels for 19% -> 21%
where the time goes in v3:
time: 104 us
  Pallas kernels  39.2 us (38%)
  blocking collectives  24.9 us (24%)
  starting transfers between devices  19.9 us (19%)
  waiting for transfers between devices  11 us (11%)
  local copies, waits for them, and re-layouts  8.39 us (8%)
    pallas_call x9, Pallas kernels, call(): pl.pallas_call(kernel, out_shape=out_shape, in_specs=[spec(n) for n in ra...  39.2 us
    all_to_all x1, blocking collectives, everywhere(): lax.all_to_all(value, ('row', 'col'), split_axis=0, concat_axis=0, tiled=...  24.9 us
    ppermute x6, starting transfers between devices, shift(): return lax.ppermute(value, ('row', 'col'), pairs)  11.8 us
    unnamed x36, local copies, waits for them, and re-layouts  8.39 us
    all_to_all x1, waiting for transfers between devices, everywhere(): lax.all_to_all(value, ('row', 'col'), split_axis=0, concat_axis=0, tiled=...  6.38 us
    all_to_all x1, starting transfers between devices, everywhere(): lax.all_to_all(value, ('row', 'col'), split_axis=0, concat_axis=0, tiled=...  4.63 us
    all_to_all x1, starting transfers between devices, shards(): lax.all_to_all(green.reshape(ROWS, 64, K), 'row', split_axis=0, concat_ax...  3.49 us
    ppermute x6, waiting for transfers between devices, shift(): return lax.ppermute(value, ('row', 'col'), pairs)  3 us
  transfers between devices with their start and end apart: 8, of which 5 were waited for; matrix products, arithmetic and copies ran while one was open for 0% of the time, Pallas kernels for 21%

profile of v3, /device:TPU:0, one launch (start us, length us, event | category | flops | bytes accessed | tf_op | source)
XLA Modules:
  0.0 103.7 jit_solution(8096344890358601435)
XLA Ops:
  0.0 6.4 %spread_rim.1 = (f32[4,80,128]{2,1,0:T(8,128)}, f32[4,160,128]{2,1,0:T(8,128)}, f32[4,40,128]{2,1,0:T(8,128)}) custom-call(s32[1,2]{1,0:T(1,128)} %bitcast.22, s32[3,2,2048]{2,1,0:T(2,128)} %bitcast.16, f32[3,2,2048]{2,1,0:T(2,128)} %bitcast.19, f32[2,2048]{1,0:T(2,128)} %charge_hbm.1), custom_call_target="tpu_custom_call" | custom-call | flops 6000000000 | bytes 688136 | tf_op jit(solution)/shard_map/spread_rim/pallas_call | solution.py:455
  6.5 8.3 %collective-permute-start.2 = (f32[4,40,128]{2,1,0:T(8,128)}, f32[4,40,128]{2,1,0:T(8,128)S(1)}, u32[]{:S(2)}, u32[]{:S(2)}) collective-permute-start(f32[4,40,128]{2,1,0:T(8,128)} %get-tuple-element.26), channel_id=1, source_target_pairs={{0,127},{1,112},{2,113},{3,114},{4,115},{5,116},{6,117},{7,118},{8... | collective-permute-start | bytes 245768 | tf_op jit(solution)/shard_map/ppermute | solution.py:476
  15.0 2.1 %collective-permute-start.1 = (f32[4,160,128]{2,1,0:T(8,128)}, f32[4,160,128]{2,1,0:T(8,128)S(1)}, u32[]{:S(2)}, u32[]{:S(2)}) collective-permute-start(f32[4,160,128]{2,1,0:T(8,128)} %get-tuple-element.25), channel_id=1, source_target_pairs={{0,15},{1,0},{2,1},{3,2},{4,3},{5,4},{6,5},{7,6},{8,7},{9,8},{10,9... | collective-permute-start | bytes 983048 | tf_op jit(solution)/shard_map/ppermute | solution.py:476
  17.1 1.0 green.1
  18.1 3.5 %all-to-all-start.1 = ((f32[8,64,256]{2,1,0:T(8,128)}), f32[8,64,256]{2,1,0:T(8,128)S(1)}, u32[]{:S(2)}, u32[]{:S(2)}) async-start(f32[8,64,256]{2,1,0:T(8,128)} %bitcast.6), calls=%async_computation.1 | async-start | bytes 1048576 | tf_op jit(solution)/shard_map/all_to_all | solution.py:517
  21.6 5.7 %spread.1.mesh_ref = f32[4,512,128]{2,1,0:T(8,128)S(1)} custom-call(s32[1,2]{1,0:T(1,128)S(1)} %bitcast.23, s32[3,2,2048]{2,1,0:T(2,128)S(1)} %bitcast.17, f32[3,2,2048]{2,1,0:T(2,128)S(1)} %bitcast.20, f32[2,2048]{1,0:T(2,128)S(1)} %copy-done.3), custom_call_target="tpu_custom_call" | custom-call | flops 8000000000 | bytes 1163272 | tf_op jit(solution)/shard_map/spread/pallas_call | solution.py:455
  27.4 1.5 %forward_z.1 = f32[2048,128]{1,0:T(8,128)S(1)} custom-call(f32[4,512,128]{2,1,0:T(8,128)S(1)} %spread.1.mesh_ref, f32[4,80,128]{2,1,0:T(8,128)S(1)} %collective-permute-done.xr_ref, f32[4,160,128]{2,1,0:T(8,128)S(1)} %collective-permute-done.1.yr_ref, f32[4,40,128]{2,1,0:T(8,128)S(1)} %collective-permute-done.2.cr_ref, bf16[4,256,256]{2,1,0:T(8,128)(2,1)S(1)} %copy-done.6), custom_call_target="tpu_custom_call" | custom-call | flops 3000000000 | bytes 3194880 | tf_op jit(solution)/shard_map/forward_z/pallas_call | solution.py:455
  28.8 1.7 %all-to-all-done.1 = f32[8,64,256]{2,1,0:T(8,128)S(1)} async-done(((f32[8,64,256]{2,1,0:T(8,128)}), f32[8,64,256]{2,1,0:T(8,128)S(1)}, u32[]{:S(2)}, u32[]{:S(2)}) %all-to-all-start.1) | async-done | bytes 524320 | tf_op jit(solution)/shard_map/all_to_all | solution.py:517
  30.5 24.9 %all_to_all.15 = f32[128,16,128]{2,1,0:T(8,128)S(1)} all-to-all(f32[128,16,128]{2,1,0:T(8,128)S(1)} %bitcast.12), channel_id=1, replica_groups=mesh['row'=8,'col'=16] {'row','col'}, dimensions={0} | all-to-all | bytes 2097152 | tf_op jit(solution)/shard_map/all_to_all | solution.py:480
  55.4 5.2 %planes.1 = f32[2048,128]{1,0:T(8,128)} custom-call(f32[2048,128]{1,0:T(8,128)S(1)} %bitcast.13, f32[512,256]{1,0:T(8,128)S(1)} %bitcast.15, bf16[4,512,512]{2,1,0:T(8,128)(2,1)S(1)} %copy-done.5, bf16[4,256,256]{2,1,0:T(8,128)(2,1)S(1)} %copy-done.7), custom_call_target="tpu_custom_call" | custom-call | flops 6000000000 | bytes 5242880 | tf_op jit(solution)/shard_map/planes/pallas_call | solution.py:455
  60.6 4.6 %all-to-all-start.2 = ((f32[128,16,128]{2,1,0:T(8,128)}), f32[128,16,128]{2,1,0:T(8,128)S(1)}, u32[]{:S(2)}, u32[]{:S(2)}) async-start(f32[128,16,128]{2,1,0:T(8,128)} %bitcast.8), calls=%async_computation.2 | async-start | bytes 2097152 | tf_op jit(solution)/shard_map/all_to_all | solution.py:480
  65.2 5.8 %weights.1 = (bf16[2,256,2048]{2,1,0:T(8,128)(2,1)S(1)}, bf16[2,256,2048]{2,1,0:T(8,128)(2,1)S(1)}, bf16[2,256,2048]{2,1,0:T(8,128)(2,1)S(1)}, bf16[2,256,2048]{2,1,0:T(8,128)(2,1)S(1)}, f32[2,128,2048]{2,1,0:T(8,128)S(1)}) custom-call(s32[1,2]{1,0:T(1,128)S(1)} %bitcast.24, s32[3,2,2048]{2,1,0:T(2,128)S(1)} %bitcast.18, f32[3,2,2048]{2,1,0:T(2,128)S(1)} %bitcast.21, ...), custom_call_target="tpu_custom_call" | custom-call | flops 10000000000 | bytes 10600456 | tf_op jit(solution)/shard_map/weights/pallas_call | solution.py:455
  71.0 1.3 %copy-done.8 = bf16[2,256,2048]{2,1,0:T(8,128)(2,1)} copy-done((bf16[2,256,2048]{2,1,0:T(8,128)(2,1)}, bf16[2,256,2048]{2,1,0:T(8,128)(2,1)S(1)}, u32[]{:S(2)}) %copy-start.8) | copy-done | bytes 2097176
  72.3 1.4 %copy-done.10 = bf16[2,256,2048]{2,1,0:T(8,128)(2,1)} copy-done((bf16[2,256,2048]{2,1,0:T(8,128)(2,1)}, bf16[2,256,2048]{2,1,0:T(8,128)(2,1)S(1)}, u32[]{:S(2)}) %copy-start.10) | copy-done | bytes 2097176
  73.6 1.4 %copy-done.12 = bf16[2,256,2048]{2,1,0:T(8,128)(2,1)} copy-done((bf16[2,256,2048]{2,1,0:T(8,128)(2,1)}, bf16[2,256,2048]{2,1,0:T(8,128)(2,1)S(1)}, u32[]{:S(2)}) %copy-start.12) | copy-done | bytes 2097176
  75.0 1.4 %copy-done.14 = bf16[2,256,2048]{2,1,0:T(8,128)(2,1)} copy-done((bf16[2,256,2048]{2,1,0:T(8,128)(2,1)}, bf16[2,256,2048]{2,1,0:T(8,128)(2,1)S(1)}, u32[]{:S(2)}) %copy-start.14) | copy-done | bytes 2097176
  76.4 1.4 %copy-done.16 = f32[2,128,2048]{2,1,0:T(8,128)} copy-done((f32[2,128,2048]{2,1,0:T(8,128)}, f32[2,128,2048]{2,1,0:T(8,128)S(1)}, u32[]{:S(2)}) %copy-start.16) | copy-done | bytes 2097176
  77.8 6.4 %all-to-all-done.2 = f32[128,16,128]{2,1,0:T(8,128)S(1)} async-done(((f32[128,16,128]{2,1,0:T(8,128)}), f32[128,16,128]{2,1,0:T(8,128)S(1)}, u32[]{:S(2)}, u32[]{:S(2)}) %all-to-all-start.2) | async-done | bytes 1048608 | tf_op jit(solution)/shard_map/all_to_all | solution.py:480
  84.2 1.3 %inverse_z.1 = (bf16[2,512,256]{2,1,0:T(8,128)(2,1)S(1)}, bf16[2,512,256]{2,1,0:T(8,128)(2,1)S(1)}, f32[4,80,128]{2,1,0:T(8,128)S(1)}, f32[4,160,128]{2,1,0:T(8,128)S(1)}, f32[4,40,128]{2,1,0:T(8,128)S(1)}) custom-call(f32[2048,128]{1,0:T(8,128)S(1)} %bitcast.11, bf16[4,256,256]{2,1,0:T(8,128)(2,1)S(1)} %copy-done.6), custom_call_target="tpu_custom_call" | custom-call | flops 3000000000 | bytes 3194880 | tf_op jit(solution)/shard_map/inverse_z/pallas_call | solution.py:455
  85.5 0.9 collective-permute-start.3
  87.0 0.6 copy-done.15
  88.2 7.3 %gather.1.inner_ref = f32[3,2,2048]{2,1,0:T(2,128)S(1)} custom-call(f32[2,128,2048]{2,1,0:T(8,128)S(1)} %copy-done.17, bf16[2,256,2048]{2,1,0:T(8,128)(2,1)S(1)} %copy-done.9, bf16[2,256,2048]{2,1,0:T(8,128)(2,1)S(1)} %copy-done.11, bf16[2,256,2048]{2,1,0:T(8,128)(2,1)S(1)} %copy-done.13, bf16[2,256,2048]{2,1,0:T(8,128)(2,1)S(1)} %copy-done.15, ...), custom_call_target="tpu_custom_call" | custom-call | flops 12000000000 | bytes 11583488 | tf_op jit(solution)/shard_map/gather/pallas_call | solution.py:455
  95.7 2.8 %collective-permute-done.4.yr_ref = f32[4,160,128]{2,1,0:T(8,128)S(1)} collective-permute-done((f32[4,160,128]{2,1,0:T(8,128)S(1)}, f32[4,160,128]{2,1,0:T(8,128)S(1)}, u32[]{:S(2)}, u32[]{:S(2)}) %collective-permute-start.4) | collective-permute-done | bytes 327712 | tf_op jit(solution)/shard_map/ppermute | solution.py:476
  98.5 5.2 %gather_rim.1 = f32[3,2,2048]{2,1,0:T(2,128)} custom-call(f32[2,128,2048]{2,1,0:T(8,128)S(1)} %copy-done.17, bf16[2,256,2048]{2,1,0:T(8,128)(2,1)S(1)} %copy-done.9, bf16[2,256,2048]{2,1,0:T(8,128)(2,1)S(1)} %copy-done.11, bf16[2,256,2048]{2,1,0:T(8,128)(2,1)S(1)} %copy-done.13, bf16[2,256,2048]{2,1,0:T(8,128)(2,1)S(1)} %copy-done.15, ...), custom_call_target="tpu_custom_call" | custom-call | flops 8000000000 | bytes 11157504 | tf_op jit(solution)/shard_map/gather_rim/pallas_call | solution.py:455
  (38 shorter events, 1.7 us)
Async XLA Ops:
  0.0 17.1 %copy-start = (f32[32,16,256]{2,1,0:T(8,128)S(1)}, f32[32,16,256]{2,1,0:T(8,128)}, u32[]{:S(2)}) copy-start(f32[32,16,256]{2,1,0:T(8,128)} %param.12) | copy-start | bytes 1572868
  6.4 15.2 %copy-start.1 = (s32[2,3,2048]{2,0,1:T(2,128)S(1)}, s32[2,3,2048]{2,0,1:T(2,128)}, u32[]{:S(2)}) copy-start(s32[2,3,2048]{2,0,1:T(2,128)} %param.8) | copy-start | bytes 147460
  6.4 15.2 %copy-start.2 = (f32[2,3,2048]{2,0,1:T(2,128)S(1)}, f32[2,3,2048]{2,0,1:T(2,128)}, u32[]{:S(2)}) copy-start(f32[2,3,2048]{2,0,1:T(2,128)} %param.9) | copy-start | bytes 147460
  6.4 15.2 %copy-start.3 = (f32[2,2048]{1,0:T(2,128)S(1)}, f32[2,2048]{1,0:T(2,128)}, u32[]{:S(2)}) copy-start(f32[2,2048]{1,0:T(2,128)} %charge_hbm.1) | copy-start | bytes 49156
  6.4 15.2 %copy-start.4 = (s32[2,1]{0,1:T(1,128)S(1)}, s32[2,1]{0,1:T(1,128)}, u32[]{:S(2)}) copy-start(s32[2,1]{0,1:T(1,128)} %param.11) | copy-start | bytes 28
  6.5 20.9 %collective-permute-start.2 = (f32[4,40,128]{2,1,0:T(8,128)}, f32[4,40,128]{2,1,0:T(8,128)S(1)}, u32[]{:S(2)}, u32[]{:S(2)}) collective-permute-start(f32[4,40,128]{2,1,0:T(8,128)} %get-tuple-element.26), channel_id=1, source_target_pairs={{0,127},{1,112},{2,113},{3,114},{4,115},{5,116},{6,117},{7,118},{8... | collective-permute-start | bytes 245768 | tf_op jit(solution)/shard_map/ppermute | solution.py:476
  14.8 12.6 %collective-permute-start = (f32[4,80,128]{2,1,0:T(8,128)}, f32[4,80,128]{2,1,0:T(8,128)S(1)}, u32[]{:S(2)}, u32[]{:S(2)}) collective-permute-start(f32[4,80,128]{2,1,0:T(8,128)} %get-tuple-element.24), channel_id=1, source_target_pairs={{0,112},{1,113},{2,114},{3,115},{4,116},{5,117},{6,118},{7,119},{8... | collective-permute-start | bytes 491528 | tf_op jit(solution)/shard_map/ppermute | solution.py:476
  15.0 12.3 %collective-permute-start.1 = (f32[4,160,128]{2,1,0:T(8,128)}, f32[4,160,128]{2,1,0:T(8,128)S(1)}, u32[]{:S(2)}, u32[]{:S(2)}) collective-permute-start(f32[4,160,128]{2,1,0:T(8,128)} %get-tuple-element.25), channel_id=1, source_target_pairs={{0,15},{1,0},{2,1},{3,2},{4,3},{5,4},{6,5},{7,6},{8,7},{9,8},{10,9... | collective-permute-start | bytes 983048 | tf_op jit(solution)/shard_map/ppermute | solution.py:476
  18.1 12.4 %all-to-all-start.1 = ((f32[8,64,256]{2,1,0:T(8,128)}), f32[8,64,256]{2,1,0:T(8,128)S(1)}, u32[]{:S(2)}, u32[]{:S(2)}) async-start(f32[8,64,256]{2,1,0:T(8,128)} %bitcast.6), calls=%async_computation.1 | async-start | bytes 1048576 | tf_op jit(solution)/shard_map/all_to_all | solution.py:517
  21.6 5.7 %copy-start.6 = (bf16[4,256,256]{2,1,0:T(8,128)(2,1)S(1)}, bf16[4,256,256]{2,1,0:T(8,128)(2,1)}, u32[]{:S(2)}) copy-start(bf16[4,256,256]{2,1,0:T(8,128)(2,1)} %constant.6.clone.zc) | copy-start | bytes 1572868
  27.4 28.1 %copy-start.7 = (bf16[4,256,256]{2,1,0:T(8,128)(2,1)S(1)}, bf16[4,256,256]{2,1,0:T(8,128)(2,1)}, u32[]{:S(2)}) copy-start(bf16[4,256,256]{2,1,0:T(8,128)(2,1)} %constant.7.clone.xc) | copy-start | bytes 1572868
  30.5 24.9 %copy-start.5 = (bf16[4,512,512]{2,1,0:T(8,128)(2,1)S(1)}, bf16[4,512,512]{2,1,0:T(8,128)(2,1)}, u32[]{:S(2)}) copy-start(bf16[4,512,512]{2,1,0:T(8,128)(2,1)} %constant.8.clone.yc) | copy-start | bytes 6291460
  60.6 23.6 %all-to-all-start.2 = ((f32[128,16,128]{2,1,0:T(8,128)}), f32[128,16,128]{2,1,0:T(8,128)S(1)}, u32[]{:S(2)}, u32[]{:S(2)}) async-start(f32[128,16,128]{2,1,0:T(8,128)} %bitcast.8), calls=%async_computation.2 | async-start | bytes 2097152 | tf_op jit(solution)/shard_map/all_to_all | solution.py:480
  72.3 1.4 %copy-start.10 = (bf16[2,256,2048]{2,1,0:T(8,128)(2,1)}, bf16[2,256,2048]{2,1,0:T(8,128)(2,1)S(1)}, u32[]{:S(2)}) copy-start(bf16[2,256,2048]{2,1,0:T(8,128)(2,1)S(1)} %get-tuple-element.21.wl_ref) | copy-start | bytes 6291460
  73.6 1.4 %copy-start.12 = (bf16[2,256,2048]{2,1,0:T(8,128)(2,1)}, bf16[2,256,2048]{2,1,0:T(8,128)(2,1)S(1)}, u32[]{:S(2)}) copy-start(bf16[2,256,2048]{2,1,0:T(8,128)(2,1)S(1)} %get-tuple-element.22.sh_ref) | copy-start | bytes 6291460
  75.0 1.4 %copy-start.14 = (bf16[2,256,2048]{2,1,0:T(8,128)(2,1)}, bf16[2,256,2048]{2,1,0:T(8,128)(2,1)S(1)}, u32[]{:S(2)}) copy-start(bf16[2,256,2048]{2,1,0:T(8,128)(2,1)S(1)} %get-tuple-element.23.sl_ref) | copy-start | bytes 6291460
  84.1 2.5 %copy-start.9 = (bf16[2,256,2048]{2,1,0:T(8,128)(2,1)S(1)}, bf16[2,256,2048]{2,1,0:T(8,128)(2,1)}, u32[]{:S(2)}) copy-start(bf16[2,256,2048]{2,1,0:T(8,128)(2,1)} %copy-done.8) | copy-start | bytes 6291460
  84.1 2.5 %copy-start.11 = (bf16[2,256,2048]{2,1,0:T(8,128)(2,1)S(1)}, bf16[2,256,2048]{2,1,0:T(8,128)(2,1)}, u32[]{:S(2)}) copy-start(bf16[2,256,2048]{2,1,0:T(8,128)(2,1)} %copy-done.10) | copy-start | bytes 6291460
  84.1 2.9 %copy-start.13 = (bf16[2,256,2048]{2,1,0:T(8,128)(2,1)S(1)}, bf16[2,256,2048]{2,1,0:T(8,128)(2,1)}, u32[]{:S(2)}) copy-start(bf16[2,256,2048]{2,1,0:T(8,128)(2,1)} %copy-done.12) | copy-start | bytes 6291460
  84.1 3.5 %copy-start.15 = (bf16[2,256,2048]{2,1,0:T(8,128)(2,1)S(1)}, bf16[2,256,2048]{2,1,0:T(8,128)(2,1)}, u32[]{:S(2)}) copy-start(bf16[2,256,2048]{2,1,0:T(8,128)(2,1)} %copy-done.14) | copy-start | bytes 6291460
  84.2 4.1 %copy-start.17 = (f32[2,128,2048]{2,1,0:T(8,128)S(1)}, f32[2,128,2048]{2,1,0:T(8,128)}, u32[]{:S(2)}) copy-start(f32[2,128,2048]{2,1,0:T(8,128)} %copy-done.16) | copy-start | bytes 6291460
  85.4 10.2 %collective-permute-start.5 = (f32[4,40,128]{2,1,0:T(8,128)S(1)}, f32[4,40,128]{2,1,0:T(8,128)S(1)}, u32[]{:S(2)}, u32[]{:S(2)}) collective-permute-start(f32[4,40,128]{2,1,0:T(8,128)S(1)} %get-tuple-element.30), channel_id=1, source_target_pairs={{0,17},{1,18},{2,19},{3,20},{4,21},{5,22},{6,23},{7,24},{8,25},{9,... | collective-permute-start | bytes 245768 | tf_op jit(solution)/shard_map/ppermute | solution.py:476
  85.5 10.2 %collective-permute-start.3 = (f32[4,80,128]{2,1,0:T(8,128)S(1)}, f32[4,80,128]{2,1,0:T(8,128)S(1)}, u32[]{:S(2)}, u32[]{:S(2)}) collective-permute-start(f32[4,80,128]{2,1,0:T(8,128)S(1)} %get-tuple-element.28), channel_id=1, source_target_pairs={{0,16},{1,17},{2,18},{3,19},{4,20},{5,21},{6,22},{7,23},{8,24},{9,... | collective-permute-start | bytes 491528 | tf_op jit(solution)/shard_map/ppermute | solution.py:476
  86.4 12.1 %collective-permute-start.4 = (f32[4,160,128]{2,1,0:T(8,128)S(1)}, f32[4,160,128]{2,1,0:T(8,128)S(1)}, u32[]{:S(2)}, u32[]{:S(2)}) collective-permute-start(f32[4,160,128]{2,1,0:T(8,128)S(1)} %get-tuple-element.29), channel_id=1, source_target_pairs={{0,1},{1,2},{2,3},{3,4},{4,5},{5,6},{6,7},{7,8},{8,9},{9,10},{10,1... | collective-permute-start | bytes 983048 | tf_op jit(solution)/shard_map/ppermute | solution.py:476
  (2 other events, 2.7 us)

commit v4 on v3

--- a/solution.py
+++ b/solution.py
@@ -387,7 +387,7 @@
         body(at, pl.ds(at, CHUNK))
         return carry
 
-    lax.fori_loop(0, ATOMS // CHUNK, step, 0)
+    lax.fori_loop(0, ATOMS // CHUNK, step, 0, unroll=2)
 
 
 def gather_kernel(xy_ref, wh_ref, wl_ref, sh_ref, sl_ref, fh_ref, fl_ref, out_ref):
@@ -528,7 +528,8 @@
     )
     packed = everywhere(packed.reshape(DEV, 16, 128)).reshape(DEV * 16, 128)
     wh, wl, gh, gl, xy = call(
-        weight_kernel, "weights", 1e10, [weights] * 4 + [shape(2, SIDES, ATOMS)], atoms, smem=(0,)
+        weight_kernel, "weights", 1e10, [weights] * 4 + [shape(2, SIDES, ATOMS)], atoms, smem=(0,),
+        limit=60,
     )
     packed = call(
         plane_kernel, "planes", 6e9, shape(DEV * 16, 128), (packed, green, yc, xc),

time: 104 us -> 104 us (level)
  local copies, waits for them, and re-layouts: 8.39 us -> 1.4 us
  waiting for transfers between devices: 11 us -> 15.8 us
  Pallas kernels: 39.2 us -> 41.1 us
    unnamed x36 -> x26, local copies, waits for them, and re-layouts: 8.39 us -> 1.4 us
    all_to_all x1, waiting for transfers between devices: 6.38 us -> 10.6 us  [everywhere(): lax.all_to_all(value, ('row', 'col'), split_axis=0, concat_axis=0, tiled=...]
    pallas_call x9, Pallas kernels: 39.2 us -> 41.1 us  [call(): pl.pallas_call(kernel, out_shape=out_shape, in_specs=[spec(n) for n in ra...]
  transfers between devices with their start and end apart: 8 -> 8, of which waited for: 5 -> 5; matrix products, arithmetic and copies ran while one was open for 0% -> 0% of each run, Pallas kernels for 21% -> 23%
where the time goes in v4:
time: 104 us
  Pallas kernels  41.1 us (40%)
  blocking collectives  24.9 us (24%)
  starting transfers between devices  20.1 us (19%)
  waiting for transfers between devices  15.8 us (15%)
  local copies, waits for them, and re-layouts  1.4 us (1%)
    pallas_call x9, Pallas kernels, call(): pl.pallas_call(kernel, out_shape=out_shape, in_specs=[spec(n) for n in ra...  41.1 us
    all_to_all x1, blocking collectives, everywhere(): lax.all_to_all(value, ('row', 'col'), split_axis=0, concat_axis=0, tiled=...  24.9 us
    ppermute x6, starting transfers between devices, shift(): return lax.ppermute(value, ('row', 'col'), pairs)  12 us
    all_to_all x1, waiting for transfers between devices, everywhere(): lax.all_to_all(value, ('row', 'col'), split_axis=0, concat_axis=0, tiled=...  10.6 us
    all_to_all x1, starting transfers between devices, everywhere(): lax.all_to_all(value, ('row', 'col'), split_axis=0, concat_axis=0, tiled=...  4.63 us
    ppermute x6, waiting for transfers between devices, shift(): return lax.ppermute(value, ('row', 'col'), pairs)  3.55 us
    all_to_all x1, starting transfers between devices, shards(): lax.all_to_all(green.reshape(ROWS, 64, K), 'row', split_axis=0, concat_ax...  3.49 us
  transfers between devices with their start and end apart: 8, of which 5 were waited for; matrix products, arithmetic and copies ran while one was open for 0% of the time, Pallas kernels for 23%

profile of v4, /device:TPU:0, one launch (start us, length us, event | category | flops | bytes accessed | tf_op | source)
XLA Modules:
  0.0 103.6 jit_solution(18281212792356298598)
XLA Ops:
  0.0 6.4 %spread_rim.1 = (f32[4,80,128]{2,1,0:T(8,128)}, f32[4,160,128]{2,1,0:T(8,128)}, f32[4,40,128]{2,1,0:T(8,128)}) custom-call(s32[1,2]{1,0:T(1,128)} %bitcast.22, s32[3,2,2048]{2,1,0:T(2,128)} %bitcast.16, f32[3,2,2048]{2,1,0:T(2,128)} %bitcast.19, f32[2,2048]{1,0:T(2,128)} %charge_hbm.1), custom_call_target="tpu_custom_call" | custom-call | flops 6000000000 | bytes 688136 | tf_op jit(solution)/shard_map/spread_rim/pallas_call | solution.py:455
  6.5 8.3 %collective-permute-start.2 = (f32[4,40,128]{2,1,0:T(8,128)}, f32[4,40,128]{2,1,0:T(8,128)S(1)}, u32[]{:S(2)}, u32[]{:S(2)}) collective-permute-start(f32[4,40,128]{2,1,0:T(8,128)} %get-tuple-element.26), channel_id=1, source_target_pairs={{0,127},{1,112},{2,113},{3,114},{4,115},{5,116},{6,117},{7,118},{8... | collective-permute-start | bytes 245768 | tf_op jit(solution)/shard_map/ppermute | solution.py:476
  14.8 0.2 collective-permute-start
  15.0 2.1 %collective-permute-start.1 = (f32[4,160,128]{2,1,0:T(8,128)}, f32[4,160,128]{2,1,0:T(8,128)S(1)}, u32[]{:S(2)}, u32[]{:S(2)}) collective-permute-start(f32[4,160,128]{2,1,0:T(8,128)} %get-tuple-element.25), channel_id=1, source_target_pairs={{0,15},{1,0},{2,1},{3,2},{4,3},{5,4},{6,5},{7,6},{8,7},{9,8},{10,9... | collective-permute-start | bytes 983048 | tf_op jit(solution)/shard_map/ppermute | solution.py:476
  17.1 1.0 green.1
  18.1 3.5 %all-to-all-start.1 = ((f32[8,64,256]{2,1,0:T(8,128)}), f32[8,64,256]{2,1,0:T(8,128)S(1)}, u32[]{:S(2)}, u32[]{:S(2)}) async-start(f32[8,64,256]{2,1,0:T(8,128)} %bitcast.6), calls=%async_computation.1 | async-start | bytes 1048576 | tf_op jit(solution)/shard_map/all_to_all | solution.py:517
  21.6 5.7 %spread.1.mesh_ref = f32[4,512,128]{2,1,0:T(8,128)S(1)} custom-call(s32[1,2]{1,0:T(1,128)S(1)} %bitcast.24, s32[3,2,2048]{2,1,0:T(2,128)S(1)} %bitcast.18, f32[3,2,2048]{2,1,0:T(2,128)S(1)} %bitcast.21, f32[2,2048]{1,0:T(2,128)S(1)} %copy-done.3), custom_call_target="tpu_custom_call" | custom-call | flops 8000000000 | bytes 1163272 | tf_op jit(solution)/shard_map/spread/pallas_call | solution.py:455
  27.3 1.5 %forward_z.1 = f32[2048,128]{1,0:T(8,128)S(1)} custom-call(f32[4,512,128]{2,1,0:T(8,128)S(1)} %spread.1.mesh_ref, f32[4,80,128]{2,1,0:T(8,128)S(1)} %collective-permute-done.xr_ref, f32[4,160,128]{2,1,0:T(8,128)S(1)} %collective-permute-done.1.yr_ref, f32[4,40,128]{2,1,0:T(8,128)S(1)} %collective-permute-done.2.cr_ref, bf16[4,256,256]{2,1,0:T(8,128)(2,1)S(1)} %copy-done.6), custom_call_target="tpu_custom_call" | custom-call | flops 3000000000 | bytes 3194880 | tf_op jit(solution)/shard_map/forward_z/pallas_call | solution.py:455
  28.8 1.7 %all-to-all-done.1 = f32[8,64,256]{2,1,0:T(8,128)S(1)} async-done(((f32[8,64,256]{2,1,0:T(8,128)}), f32[8,64,256]{2,1,0:T(8,128)S(1)}, u32[]{:S(2)}, u32[]{:S(2)}) %all-to-all-start.1) | async-done | bytes 524320 | tf_op jit(solution)/shard_map/all_to_all | solution.py:517
  30.5 24.9 %all_to_all.15 = f32[128,16,128]{2,1,0:T(8,128)S(1)} all-to-all(f32[128,16,128]{2,1,0:T(8,128)S(1)} %bitcast.12), channel_id=1, replica_groups=mesh['row'=8,'col'=16] {'row','col'}, dimensions={0} | all-to-all | bytes 2097152 | tf_op jit(solution)/shard_map/all_to_all | solution.py:480
  55.4 5.2 %planes.1 = f32[2048,128]{1,0:T(8,128)} custom-call(f32[2048,128]{1,0:T(8,128)S(1)} %bitcast.13, f32[512,256]{1,0:T(8,128)S(1)} %bitcast.15, bf16[4,512,512]{2,1,0:T(8,128)(2,1)S(1)} %copy-done.5, bf16[4,256,256]{2,1,0:T(8,128)(2,1)S(1)} %copy-done.7), custom_call_target="tpu_custom_call" | custom-call | flops 6000000000 | bytes 5242880 | tf_op jit(solution)/shard_map/planes/pallas_call | solution.py:455
  60.6 4.6 %all-to-all-start.2 = ((f32[128,16,128]{2,1,0:T(8,128)}), f32[128,16,128]{2,1,0:T(8,128)S(1)}, u32[]{:S(2)}, u32[]{:S(2)}) async-start(f32[128,16,128]{2,1,0:T(8,128)} %bitcast.8), calls=%async_computation.2 | async-start | bytes 2097152 | tf_op jit(solution)/shard_map/all_to_all | solution.py:480
  65.2 8.3 %weights.1 = (bf16[2,256,2048]{2,1,0:T(8,128)(2,1)}, bf16[2,256,2048]{2,1,0:T(8,128)(2,1)}, bf16[2,256,2048]{2,1,0:T(8,128)(2,1)}, bf16[2,256,2048]{2,1,0:T(8,128)(2,1)}, f32[2,128,2048]{2,1,0:T(8,128)}) custom-call(s32[1,2]{1,0:T(1,128)} %bitcast.23, s32[3,2,2048]{2,1,0:T(2,128)} %bitcast.17, f32[3,2,2048]{2,1,0:T(2,128)} %bitcast.20, f32[2,2048]{1,0:T(2,128)} %charge_hbm.1), custom_call_target="tpu_custom_call" | custom-call | flops 10000000000 | bytes 10600456 | tf_op jit(solution)/shard_map/weights/pallas_call | solution.py:455
  73.5 10.6 %all-to-all-done.2 = f32[128,16,128]{2,1,0:T(8,128)S(1)} async-done(((f32[128,16,128]{2,1,0:T(8,128)}), f32[128,16,128]{2,1,0:T(8,128)S(1)}, u32[]{:S(2)}, u32[]{:S(2)}) %all-to-all-start.2) | async-done | bytes 1048608 | tf_op jit(solution)/shard_map/all_to_all | solution.py:480
  84.2 1.3 %inverse_z.1 = (bf16[2,512,256]{2,1,0:T(8,128)(2,1)S(1)}, bf16[2,512,256]{2,1,0:T(8,128)(2,1)S(1)}, f32[4,80,128]{2,1,0:T(8,128)S(1)}, f32[4,160,128]{2,1,0:T(8,128)S(1)}, f32[4,40,128]{2,1,0:T(8,128)S(1)}) custom-call(f32[2048,128]{1,0:T(8,128)S(1)} %bitcast.11, bf16[4,256,256]{2,1,0:T(8,128)(2,1)S(1)} %copy-done.6), custom_call_target="tpu_custom_call" | custom-call | flops 3000000000 | bytes 3194880 | tf_op jit(solution)/shard_map/inverse_z/pallas_call | solution.py:455
  85.5 0.3 collective-permute-start.5
  85.8 0.9 collective-permute-start.3
  86.6 0.2 collective-permute-start.4
  87.0 0.6 copy-done.11
  87.6 0.6 copy-done.12
  88.2 7.0 %gather.1.inner_ref = f32[3,2,2048]{2,1,0:T(2,128)S(1)} custom-call(f32[2,128,2048]{2,1,0:T(8,128)S(1)} %copy-done.12, bf16[2,256,2048]{2,1,0:T(8,128)(2,1)S(1)} %copy-done.8, bf16[2,256,2048]{2,1,0:T(8,128)(2,1)S(1)} %copy-done.9, bf16[2,256,2048]{2,1,0:T(8,128)(2,1)S(1)} %copy-done.10, bf16[2,256,2048]{2,1,0:T(8,128)(2,1)S(1)} %copy-done.11, ...), custom_call_target="tpu_custom_call" | custom-call | flops 12000000000 | bytes 11583488 | tf_op jit(solution)/shard_map/gather/pallas_call | solution.py:455
  95.2 0.7 collective-permute-done.5.cr_ref
  96.0 2.8 %collective-permute-done.4.yr_ref = f32[4,160,128]{2,1,0:T(8,128)S(1)} collective-permute-done((f32[4,160,128]{2,1,0:T(8,128)S(1)}, f32[4,160,128]{2,1,0:T(8,128)S(1)}, u32[]{:S(2)}, u32[]{:S(2)}) %collective-permute-start.4) | collective-permute-done | bytes 327712 | tf_op jit(solution)/shard_map/ppermute | solution.py:476
  98.8 4.8 %gather_rim.1 = f32[3,2,2048]{2,1,0:T(2,128)} custom-call(f32[2,128,2048]{2,1,0:T(8,128)S(1)} %copy-done.12, bf16[2,256,2048]{2,1,0:T(8,128)(2,1)S(1)} %copy-done.8, bf16[2,256,2048]{2,1,0:T(8,128)(2,1)S(1)} %copy-done.9, bf16[2,256,2048]{2,1,0:T(8,128)(2,1)S(1)} %copy-done.10, bf16[2,256,2048]{2,1,0:T(8,128)(2,1)S(1)} %copy-done.11, ...), custom_call_target="tpu_custom_call" | custom-call | flops 8000000000 | bytes 11157504 | tf_op jit(solution)/shard_map/gather_rim/pallas_call | solution.py:455
  (28 shorter events, 0.3 us)
Async XLA Ops:
  0.0 17.1 %copy-start = (f32[32,16,256]{2,1,0:T(8,128)S(1)}, f32[32,16,256]{2,1,0:T(8,128)}, u32[]{:S(2)}) copy-start(f32[32,16,256]{2,1,0:T(8,128)} %param.12) | copy-start | bytes 1572868
  6.4 15.1 %copy-start.1 = (s32[2,3,2048]{2,0,1:T(2,128)S(1)}, s32[2,3,2048]{2,0,1:T(2,128)}, u32[]{:S(2)}) copy-start(s32[2,3,2048]{2,0,1:T(2,128)} %param.8) | copy-start | bytes 147460
  6.4 15.1 %copy-start.2 = (f32[2,3,2048]{2,0,1:T(2,128)S(1)}, f32[2,3,2048]{2,0,1:T(2,128)}, u32[]{:S(2)}) copy-start(f32[2,3,2048]{2,0,1:T(2,128)} %param.9) | copy-start | bytes 147460
  6.4 15.1 %copy-start.3 = (f32[2,2048]{1,0:T(2,128)S(1)}, f32[2,2048]{1,0:T(2,128)}, u32[]{:S(2)}) copy-start(f32[2,2048]{1,0:T(2,128)} %charge_hbm.1) | copy-start | bytes 49156
  6.5 15.1 %copy-start.4 = (s32[2,1]{0,1:T(1,128)S(1)}, s32[2,1]{0,1:T(1,128)}, u32[]{:S(2)}) copy-start(s32[2,1]{0,1:T(1,128)} %param.11) | copy-start | bytes 28
  6.5 20.8 %collective-permute-start.2 = (f32[4,40,128]{2,1,0:T(8,128)}, f32[4,40,128]{2,1,0:T(8,128)S(1)}, u32[]{:S(2)}, u32[]{:S(2)}) collective-permute-start(f32[4,40,128]{2,1,0:T(8,128)} %get-tuple-element.26), channel_id=1, source_target_pairs={{0,127},{1,112},{2,113},{3,114},{4,115},{5,116},{6,117},{7,118},{8... | collective-permute-start | bytes 245768 | tf_op jit(solution)/shard_map/ppermute | solution.py:476
  14.8 12.5 %collective-permute-start = (f32[4,80,128]{2,1,0:T(8,128)}, f32[4,80,128]{2,1,0:T(8,128)S(1)}, u32[]{:S(2)}, u32[]{:S(2)}) collective-permute-start(f32[4,80,128]{2,1,0:T(8,128)} %get-tuple-element.24), channel_id=1, source_target_pairs={{0,112},{1,113},{2,114},{3,115},{4,116},{5,117},{6,118},{7,119},{8... | collective-permute-start | bytes 491528 | tf_op jit(solution)/shard_map/ppermute | solution.py:476
  15.0 12.3 %collective-permute-start.1 = (f32[4,160,128]{2,1,0:T(8,128)}, f32[4,160,128]{2,1,0:T(8,128)S(1)}, u32[]{:S(2)}, u32[]{:S(2)}) collective-permute-start(f32[4,160,128]{2,1,0:T(8,128)} %get-tuple-element.25), channel_id=1, source_target_pairs={{0,15},{1,0},{2,1},{3,2},{4,3},{5,4},{6,5},{7,6},{8,7},{9,8},{10,9... | collective-permute-start | bytes 983048 | tf_op jit(solution)/shard_map/ppermute | solution.py:476
  18.1 12.4 %all-to-all-start.1 = ((f32[8,64,256]{2,1,0:T(8,128)}), f32[8,64,256]{2,1,0:T(8,128)S(1)}, u32[]{:S(2)}, u32[]{:S(2)}) async-start(f32[8,64,256]{2,1,0:T(8,128)} %bitcast.6), calls=%async_computation.1 | async-start | bytes 1048576 | tf_op jit(solution)/shard_map/all_to_all | solution.py:517
  21.6 5.7 %copy-start.6 = (bf16[4,256,256]{2,1,0:T(8,128)(2,1)S(1)}, bf16[4,256,256]{2,1,0:T(8,128)(2,1)}, u32[]{:S(2)}) copy-start(bf16[4,256,256]{2,1,0:T(8,128)(2,1)} %constant.6.clone.zc) | copy-start | bytes 1572868
  27.3 28.1 %copy-start.7 = (bf16[4,256,256]{2,1,0:T(8,128)(2,1)S(1)}, bf16[4,256,256]{2,1,0:T(8,128)(2,1)}, u32[]{:S(2)}) copy-start(bf16[4,256,256]{2,1,0:T(8,128)(2,1)} %constant.7.clone.xc) | copy-start | bytes 1572868
  30.5 24.9 %copy-start.5 = (bf16[4,512,512]{2,1,0:T(8,128)(2,1)S(1)}, bf16[4,512,512]{2,1,0:T(8,128)(2,1)}, u32[]{:S(2)}) copy-start(bf16[4,512,512]{2,1,0:T(8,128)(2,1)} %constant.8.clone.yc) | copy-start | bytes 6291460
  60.6 23.6 %all-to-all-start.2 = ((f32[128,16,128]{2,1,0:T(8,128)}), f32[128,16,128]{2,1,0:T(8,128)S(1)}, u32[]{:S(2)}, u32[]{:S(2)}) async-start(f32[128,16,128]{2,1,0:T(8,128)} %bitcast.8), calls=%async_computation.2 | async-start | bytes 2097152 | tf_op jit(solution)/shard_map/all_to_all | solution.py:480
  84.2 2.7 %copy-start.8 = (bf16[2,256,2048]{2,1,0:T(8,128)(2,1)S(1)}, bf16[2,256,2048]{2,1,0:T(8,128)(2,1)}, u32[]{:S(2)}) copy-start(bf16[2,256,2048]{2,1,0:T(8,128)(2,1)} %get-tuple-element.20.wh_ref) | copy-start | bytes 6291460
  84.2 2.7 %copy-start.9 = (bf16[2,256,2048]{2,1,0:T(8,128)(2,1)S(1)}, bf16[2,256,2048]{2,1,0:T(8,128)(2,1)}, u32[]{:S(2)}) copy-start(bf16[2,256,2048]{2,1,0:T(8,128)(2,1)} %get-tuple-element.21.wl_ref) | copy-start | bytes 6291460
  84.2 2.9 %copy-start.10 = (bf16[2,256,2048]{2,1,0:T(8,128)(2,1)S(1)}, bf16[2,256,2048]{2,1,0:T(8,128)(2,1)}, u32[]{:S(2)}) copy-start(bf16[2,256,2048]{2,1,0:T(8,128)(2,1)} %get-tuple-element.22.sh_ref) | copy-start | bytes 6291460
  84.2 3.5 %copy-start.11 = (bf16[2,256,2048]{2,1,0:T(8,128)(2,1)S(1)}, bf16[2,256,2048]{2,1,0:T(8,128)(2,1)}, u32[]{:S(2)}) copy-start(bf16[2,256,2048]{2,1,0:T(8,128)(2,1)} %get-tuple-element.23.sl_ref) | copy-start | bytes 6291460
  84.2 4.1 %copy-start.12 = (f32[2,128,2048]{2,1,0:T(8,128)S(1)}, f32[2,128,2048]{2,1,0:T(8,128)}, u32[]{:S(2)}) copy-start(f32[2,128,2048]{2,1,0:T(8,128)} %get-tuple-element.19.xy_ref) | copy-start | bytes 6291460
  85.5 10.4 %collective-permute-start.5 = (f32[4,40,128]{2,1,0:T(8,128)S(1)}, f32[4,40,128]{2,1,0:T(8,128)S(1)}, u32[]{:S(2)}, u32[]{:S(2)}) collective-permute-start(f32[4,40,128]{2,1,0:T(8,128)S(1)} %get-tuple-element.30), channel_id=1, source_target_pairs={{0,17},{1,18},{2,19},{3,20},{4,21},{5,22},{6,23},{7,24},{8,25},{9,... | collective-permute-start | bytes 245768 | tf_op jit(solution)/shard_map/ppermute | solution.py:476
  85.8 10.2 %collective-permute-start.3 = (f32[4,80,128]{2,1,0:T(8,128)S(1)}, f32[4,80,128]{2,1,0:T(8,128)S(1)}, u32[]{:S(2)}, u32[]{:S(2)}) collective-permute-start(f32[4,80,128]{2,1,0:T(8,128)S(1)} %get-tuple-element.28), channel_id=1, source_target_pairs={{0,16},{1,17},{2,18},{3,19},{4,20},{5,21},{6,22},{7,23},{8,24},{9,... | collective-permute-start | bytes 491528 | tf_op jit(solution)/shard_map/ppermute | solution.py:476
  86.6 12.1 %collective-permute-start.4 = (f32[4,160,128]{2,1,0:T(8,128)S(1)}, f32[4,160,128]{2,1,0:T(8,128)S(1)}, u32[]{:S(2)}, u32[]{:S(2)}) collective-permute-start(f32[4,160,128]{2,1,0:T(8,128)S(1)} %get-tuple-element.29), channel_id=1, source_target_pairs={{0,1},{1,2},{2,3},{3,4},{4,5},{5,6},{6,7},{7,8},{8,9},{9,10},{10,1... | collective-permute-start | bytes 983048 | tf_op jit(solution)/shard_map/ppermute | solution.py:476

commit v5 on v4

--- a/solution.py
+++ b/solution.py
@@ -7,6 +7,7 @@
 from jax.experimental import pallas as pl
 from jax.experimental.pallas import tpu as pltpu
 from jax.sharding import PartitionSpec as P
+
 
 F32 = jnp.float32
 BF16 = jnp.bfloat16
@@ -443,7 +444,7 @@
             out_ref[k * XB : (k + 1) * XB, lanes] = m[pl.ds(k, XB, stride=COLS), :]
 
 
-def call(kernel, name, flops, out_shape, operands, smem=(), hbm=(), scratch=(), limit=24):
+def call(kernel, flops, out_shape, operands, smem=(), hbm=(), scratch=(), limit=24):
     def spec(n):
         if n in hbm:
             return HBM_ALL
@@ -460,7 +461,6 @@
         scratch_shapes=list(scratch),
         compiler_params=pltpu.CompilerParams(vmem_limit_bytes=limit * 2**20),
         cost_estimate=pl.CostEstimate(flops=int(flops), bytes_accessed=size, transcendentals=0),
-        name=name,
     )(*operands)
 
 
@@ -476,6 +476,13 @@
     return lax.ppermute(value, ("row", "col"), pairs)
 
 
+def rims_moved(xr, yr, cr, by):
+    yr = shift(yr, 0, by)
+    xr = shift(xr, by, 0)
+    cr = shift(cr, by, by)
+    return xr, yr, cr
+
+
 def everywhere(value):
     return lax.all_to_all(value, ("row", "col"), split_axis=0, concat_axis=0, tiled=True)
 
@@ -495,7 +502,7 @@
 
     table = pltpu.VMEM((2, K, ATOMS), BF16)
     xr, yr, cr = call(
-        spread_rim_kernel, "spread_rim", 6e9, rim_shapes, atoms,
+        spread_rim_kernel, 6e9, rim_shapes, atoms,
         smem=(0,), hbm=(1, 2, 3), limit=60,
         scratch=[
             pltpu.VMEM((3, 2, ATOMS), jnp.int32),
@@ -509,45 +516,45 @@
         ],
     )
     later, _ = lax.optimization_barrier((influence, cr))
-    xr, yr, cr = shift(xr, -1, 0), shift(yr, 0, -1), shift(cr, -1, -1)
+    xr, yr, cr = rims_moved(xr, yr, cr, -1)
     green = call(
-        green_kernel, "green", 1e8, shape(512, K), (later.reshape(XB * COLS, K),),
+        green_kernel, 1e8, shape(512, K), (later.reshape(XB * COLS, K),),
         scratch=[pltpu.VMEM((512, 128), F32)],
     )
     green = lax.all_to_all(
         green.reshape(ROWS, 64, K), "row", split_axis=0, concat_axis=0, tiled=True
     ).reshape(512, K)
     mesh = call(
-        spread_kernel, "spread", 8e9, shape(4, INNER, 128), atoms,
+        spread_kernel, 8e9, shape(4, INNER, 128), atoms,
         smem=(0,), limit=32,
         scratch=[pltpu.VMEM((2, INNER, ATOMS), BF16)] * 2 + [table] * 2,
     )
     packed = call(
-        forward_z_kernel, "forward_z", 3e9, shape(DEV * 16, 128), (mesh, xr, yr, cr, zc),
+        forward_z_kernel, 3e9, shape(DEV * 16, 128), (mesh, xr, yr, cr, zc),
         scratch=[pltpu.VMEM((4, INNER, 128), F32)],
     )
     packed = everywhere(packed.reshape(DEV, 16, 128)).reshape(DEV * 16, 128)
     wh, wl, gh, gl, xy = call(
-        weight_kernel, "weights", 1e10, [weights] * 4 + [shape(2, SIDES, ATOMS)], atoms, smem=(0,),
+        weight_kernel, 1e10, [weights] * 4 + [shape(2, SIDES, ATOMS)], atoms, smem=(0,),
         limit=60,
     )
     packed = call(
-        plane_kernel, "planes", 6e9, shape(DEV * 16, 128), (packed, green, yc, xc),
+        plane_kernel, 6e9, shape(DEV * 16, 128), (packed, green, yc, xc),
         scratch=[pltpu.VMEM((2, 512, K), F32)] * 2,
     )
     packed = everywhere(packed.reshape(DEV, 16, 128)).reshape(DEV * 16, 128)
     fh, fl, xr, yr, cr = call(
-        inverse_z_kernel, "inverse_z", 3e9, [shape(2, INNER, K, dtype=BF16)] * 2 + rim_shapes,
+        inverse_z_kernel, 3e9, [shape(2, INNER, K, dtype=BF16)] * 2 + rim_shapes,
         (packed, zc),
         scratch=[pltpu.VMEM((4, INNER, 128), F32)],
     )
-    xr, yr, cr = shift(xr, 1, 0), shift(yr, 0, 1), shift(cr, 1, 1)
+    xr, yr, cr = rims_moved(xr, yr, cr, 1)
     inner = call(
-        gather_kernel, "gather", 1.2e10, shape(3, 2, ATOMS),
+        gather_kernel, 1.2e10, shape(3, 2, ATOMS),
         (xy, wh, wl, gh, gl, fh, fl),
     )
     forces = call(
-        gather_rim_kernel, "gather_rim", 8e9, shape(3, 2, ATOMS),
+        gather_rim_kernel, 8e9, shape(3, 2, ATOMS),
         (xy, wh, wl, gh, gl, xr, yr, cr, inner),
         scratch=[pltpu.VMEM((2, RIMS + 8, K), BF16)] * 2,
     )

time: 104 us -> 104 us (level)
  no operation moved by 1% of the time
where the time goes in v5:
time: 104 us
  Pallas kernels  41.1 us (40%)
  blocking collectives  24.9 us (24%)
  starting transfers between devices  20.1 us (19%)
  waiting for transfers between devices  15.8 us (15%)
  local copies, waits for them, and re-layouts  1.4 us (1%)
    pallas_call x9, Pallas kernels, call(): pl.pallas_call(kernel, out_shape=out_shape, in_specs=[spec(n) for n in ra...  41.1 us
    all_to_all x1, blocking collectives, everywhere(): lax.all_to_all(value, ('row', 'col'), split_axis=0, concat_axis=0, tiled=...  24.9 us
    ppermute x6, starting transfers between devices, shift(): return lax.ppermute(value, ('row', 'col'), pairs)  12 us
    all_to_all x1, waiting for transfers between devices, everywhere(): lax.all_to_all(value, ('row', 'col'), split_axis=0, concat_axis=0, tiled=...  10.6 us
    all_to_all x1, starting transfers between devices, everywhere(): lax.all_to_all(value, ('row', 'col'), split_axis=0, concat_axis=0, tiled=...  4.63 us
    ppermute x6, waiting for transfers between devices, shift(): return lax.ppermute(value, ('row', 'col'), pairs)  3.55 us
    all_to_all x1, starting transfers between devices, shards(): lax.all_to_all(green.reshape(ROWS, 64, K), 'row', split_axis=0, concat_ax...  3.49 us
  transfers between devices with their start and end apart: 8, of which 5 were waited for; matrix products, arithmetic and copies ran while one was open for 0% of the time, Pallas kernels for 23%

profile of v5, /device:TPU:0, one launch (start us, length us, event | category | flops | bytes accessed | tf_op | source)
XLA Modules:
  0.0 103.6 jit_solution(18281212792356298598)
XLA Ops:
  0.0 6.4 %shard_map.84 = (f32[4,80,128]{2,1,0:T(8,128)}, f32[4,160,128]{2,1,0:T(8,128)}, f32[4,40,128]{2,1,0:T(8,128)}) custom-call(s32[1,2]{1,0:T(1,128)} %bitcast.22, s32[3,2,2048]{2,1,0:T(2,128)} %bitcast.16, f32[3,2,2048]{2,1,0:T(2,128)} %bitcast.19, f32[2,2048]{1,0:T(2,128)} %charge_hbm.1), custom_call_target="tpu_custom_call" | custom-call | flops 6000000000 | bytes 688136 | tf_op jit(solution)/shard_map/pallas_call | solution.py:456
  6.5 8.3 %collective-permute-start.2 = (f32[4,40,128]{2,1,0:T(8,128)}, f32[4,40,128]{2,1,0:T(8,128)S(1)}, u32[]{:S(2)}, u32[]{:S(2)}) collective-permute-start(f32[4,40,128]{2,1,0:T(8,128)} %get-tuple-element.26), channel_id=1, source_target_pairs={{0,127},{1,112},{2,113},{3,114},{4,115},{5,116},{6,117},{7,118},{8... | collective-permute-start | bytes 245768 | tf_op jit(solution)/shard_map/ppermute | solution.py:476
  14.8 0.2 collective-permute-start
  15.0 2.1 %collective-permute-start.1 = (f32[4,160,128]{2,1,0:T(8,128)}, f32[4,160,128]{2,1,0:T(8,128)S(1)}, u32[]{:S(2)}, u32[]{:S(2)}) collective-permute-start(f32[4,160,128]{2,1,0:T(8,128)} %get-tuple-element.25), channel_id=1, source_target_pairs={{0,15},{1,0},{2,1},{3,2},{4,3},{5,4},{6,5},{7,6},{8,7},{9,8},{10,9... | collective-permute-start | bytes 983048 | tf_op jit(solution)/shard_map/ppermute | solution.py:476
  17.1 1.0 shard_map.86
  18.1 3.5 %all-to-all-start.1 = ((f32[8,64,256]{2,1,0:T(8,128)}), f32[8,64,256]{2,1,0:T(8,128)S(1)}, u32[]{:S(2)}, u32[]{:S(2)}) async-start(f32[8,64,256]{2,1,0:T(8,128)} %bitcast.6), calls=%async_computation.1 | async-start | bytes 1048576 | tf_op jit(solution)/shard_map/all_to_all | solution.py:524
  21.6 5.7 %shard_map.83.mesh_ref = f32[4,512,128]{2,1,0:T(8,128)S(1)} custom-call(s32[1,2]{1,0:T(1,128)S(1)} %bitcast.24, s32[3,2,2048]{2,1,0:T(2,128)S(1)} %bitcast.18, f32[3,2,2048]{2,1,0:T(2,128)S(1)} %bitcast.21, f32[2,2048]{1,0:T(2,128)S(1)} %copy-done.3), custom_call_target="tpu_custom_call" | custom-call | flops 8000000000 | bytes 1163272 | tf_op jit(solution)/shard_map/pallas_call | solution.py:456
  27.3 1.5 %shard_map.85 = f32[2048,128]{1,0:T(8,128)S(1)} custom-call(f32[4,512,128]{2,1,0:T(8,128)S(1)} %shard_map.83.mesh_ref, f32[4,80,128]{2,1,0:T(8,128)S(1)} %collective-permute-done.xr_ref, f32[4,160,128]{2,1,0:T(8,128)S(1)} %collective-permute-done.1.yr_ref, f32[4,40,128]{2,1,0:T(8,128)S(1)} %collective-permute-done.2.cr_ref, bf16[4,256,256]{2,1,0:T(8,128)(2,1)S(1)} %copy-done.6), custom_call_target="tpu_custom_call" | custom-call | flops 3000000000 | bytes 3194880 | tf_op jit(solution)/shard_map/pallas_call | solution.py:456
  28.8 1.7 %all-to-all-done.1 = f32[8,64,256]{2,1,0:T(8,128)S(1)} async-done(((f32[8,64,256]{2,1,0:T(8,128)}), f32[8,64,256]{2,1,0:T(8,128)S(1)}, u32[]{:S(2)}, u32[]{:S(2)}) %all-to-all-start.1) | async-done | bytes 524320 | tf_op jit(solution)/shard_map/all_to_all | solution.py:524
  30.5 24.9 %all_to_all.15 = f32[128,16,128]{2,1,0:T(8,128)S(1)} all-to-all(f32[128,16,128]{2,1,0:T(8,128)S(1)} %bitcast.12), channel_id=1, replica_groups=mesh['row'=8,'col'=16] {'row','col'}, dimensions={0} | all-to-all | bytes 2097152 | tf_op jit(solution)/shard_map/all_to_all | solution.py:487
  55.4 5.2 %shard_map.87 = f32[2048,128]{1,0:T(8,128)} custom-call(f32[2048,128]{1,0:T(8,128)S(1)} %bitcast.13, f32[512,256]{1,0:T(8,128)S(1)} %bitcast.15, bf16[4,512,512]{2,1,0:T(8,128)(2,1)S(1)} %copy-done.5, bf16[4,256,256]{2,1,0:T(8,128)(2,1)S(1)} %copy-done.7), custom_call_target="tpu_custom_call" | custom-call | flops 6000000000 | bytes 5242880 | tf_op jit(solution)/shard_map/pallas_call | solution.py:456
  60.6 4.6 %all-to-all-start.2 = ((f32[128,16,128]{2,1,0:T(8,128)}), f32[128,16,128]{2,1,0:T(8,128)S(1)}, u32[]{:S(2)}, u32[]{:S(2)}) async-start(f32[128,16,128]{2,1,0:T(8,128)} %bitcast.8), calls=%async_computation.2 | async-start | bytes 2097152 | tf_op jit(solution)/shard_map/all_to_all | solution.py:487
  65.2 8.3 %shard_map.82 = (bf16[2,256,2048]{2,1,0:T(8,128)(2,1)}, bf16[2,256,2048]{2,1,0:T(8,128)(2,1)}, bf16[2,256,2048]{2,1,0:T(8,128)(2,1)}, bf16[2,256,2048]{2,1,0:T(8,128)(2,1)}, f32[2,128,2048]{2,1,0:T(8,128)}) custom-call(s32[1,2]{1,0:T(1,128)} %bitcast.23, s32[3,2,2048]{2,1,0:T(2,128)} %bitcast.17, f32[3,2,2048]{2,1,0:T(2,128)} %bitcast.20, f32[2,2048]{1,0:T(2,128)} %charge_hbm.1), custom_call_target="tpu_custom_call" | custom-call | flops 10000000000 | bytes 10600456 | tf_op jit(solution)/shard_map/pallas_call | solution.py:456
  73.5 10.6 %all-to-all-done.2 = f32[128,16,128]{2,1,0:T(8,128)S(1)} async-done(((f32[128,16,128]{2,1,0:T(8,128)}), f32[128,16,128]{2,1,0:T(8,128)S(1)}, u32[]{:S(2)}, u32[]{:S(2)}) %all-to-all-start.2) | async-done | bytes 1048608 | tf_op jit(solution)/shard_map/all_to_all | solution.py:487
  84.2 1.3 %shard_map.88 = (bf16[2,512,256]{2,1,0:T(8,128)(2,1)S(1)}, bf16[2,512,256]{2,1,0:T(8,128)(2,1)S(1)}, f32[4,80,128]{2,1,0:T(8,128)S(1)}, f32[4,160,128]{2,1,0:T(8,128)S(1)}, f32[4,40,128]{2,1,0:T(8,128)S(1)}) custom-call(f32[2048,128]{1,0:T(8,128)S(1)} %bitcast.11, bf16[4,256,256]{2,1,0:T(8,128)(2,1)S(1)} %copy-done.6), custom_call_target="tpu_custom_call" | custom-call | flops 3000000000 | bytes 3194880 | tf_op jit(solution)/shard_map/pallas_call | solution.py:456
  85.5 0.3 collective-permute-start.5
  85.8 0.9 collective-permute-start.3
  86.6 0.2 collective-permute-start.4
  87.0 0.6 copy-done.11
  87.6 0.6 copy-done.12
  88.2 7.0 %shard_map.89.inner_ref = f32[3,2,2048]{2,1,0:T(2,128)S(1)} custom-call(f32[2,128,2048]{2,1,0:T(8,128)S(1)} %copy-done.12, bf16[2,256,2048]{2,1,0:T(8,128)(2,1)S(1)} %copy-done.8, bf16[2,256,2048]{2,1,0:T(8,128)(2,1)S(1)} %copy-done.9, bf16[2,256,2048]{2,1,0:T(8,128)(2,1)S(1)} %copy-done.10, bf16[2,256,2048]{2,1,0:T(8,128)(2,1)S(1)} %copy-done.11, ...), custom_call_target="tpu_custom_call" | custom-call | flops 12000000000 | bytes 11583488 | tf_op jit(solution)/shard_map/pallas_call | solution.py:456
  95.2 0.7 collective-permute-done.5.cr_ref
  96.0 2.8 %collective-permute-done.4.yr_ref = f32[4,160,128]{2,1,0:T(8,128)S(1)} collective-permute-done((f32[4,160,128]{2,1,0:T(8,128)S(1)}, f32[4,160,128]{2,1,0:T(8,128)S(1)}, u32[]{:S(2)}, u32[]{:S(2)}) %collective-permute-start.4) | collective-permute-done | bytes 327712 | tf_op jit(solution)/shard_map/ppermute | solution.py:476
  98.8 4.8 %shard_map.90 = f32[3,2,2048]{2,1,0:T(2,128)} custom-call(f32[2,128,2048]{2,1,0:T(8,128)S(1)} %copy-done.12, bf16[2,256,2048]{2,1,0:T(8,128)(2,1)S(1)} %copy-done.8, bf16[2,256,2048]{2,1,0:T(8,128)(2,1)S(1)} %copy-done.9, bf16[2,256,2048]{2,1,0:T(8,128)(2,1)S(1)} %copy-done.10, bf16[2,256,2048]{2,1,0:T(8,128)(2,1)S(1)} %copy-done.11, ...), custom_call_target="tpu_custom_call" | custom-call | flops 8000000000 | bytes 11157504 | tf_op jit(solution)/shard_map/pallas_call | solution.py:456
  (28 shorter events, 0.3 us)
Async XLA Ops:
  0.0 17.1 %copy-start = (f32[32,16,256]{2,1,0:T(8,128)S(1)}, f32[32,16,256]{2,1,0:T(8,128)}, u32[]{:S(2)}) copy-start(f32[32,16,256]{2,1,0:T(8,128)} %param.12) | copy-start | bytes 1572868
  6.4 15.1 %copy-start.1 = (s32[2,3,2048]{2,0,1:T(2,128)S(1)}, s32[2,3,2048]{2,0,1:T(2,128)}, u32[]{:S(2)}) copy-start(s32[2,3,2048]{2,0,1:T(2,128)} %param.8) | copy-start | bytes 147460
  6.4 15.1 %copy-start.2 = (f32[2,3,2048]{2,0,1:T(2,128)S(1)}, f32[2,3,2048]{2,0,1:T(2,128)}, u32[]{:S(2)}) copy-start(f32[2,3,2048]{2,0,1:T(2,128)} %param.9) | copy-start | bytes 147460
  6.4 15.1 %copy-start.3 = (f32[2,2048]{1,0:T(2,128)S(1)}, f32[2,2048]{1,0:T(2,128)}, u32[]{:S(2)}) copy-start(f32[2,2048]{1,0:T(2,128)} %charge_hbm.1) | copy-start | bytes 49156
  6.5 15.1 %copy-start.4 = (s32[2,1]{0,1:T(1,128)S(1)}, s32[2,1]{0,1:T(1,128)}, u32[]{:S(2)}) copy-start(s32[2,1]{0,1:T(1,128)} %param.11) | copy-start | bytes 28
  6.5 20.8 %collective-permute-start.2 = (f32[4,40,128]{2,1,0:T(8,128)}, f32[4,40,128]{2,1,0:T(8,128)S(1)}, u32[]{:S(2)}, u32[]{:S(2)}) collective-permute-start(f32[4,40,128]{2,1,0:T(8,128)} %get-tuple-element.26), channel_id=1, source_target_pairs={{0,127},{1,112},{2,113},{3,114},{4,115},{5,116},{6,117},{7,118},{8... | collective-permute-start | bytes 245768 | tf_op jit(solution)/shard_map/ppermute | solution.py:476
  14.8 12.5 %collective-permute-start = (f32[4,80,128]{2,1,0:T(8,128)}, f32[4,80,128]{2,1,0:T(8,128)S(1)}, u32[]{:S(2)}, u32[]{:S(2)}) collective-permute-start(f32[4,80,128]{2,1,0:T(8,128)} %get-tuple-element.24), channel_id=1, source_target_pairs={{0,112},{1,113},{2,114},{3,115},{4,116},{5,117},{6,118},{7,119},{8... | collective-permute-start | bytes 491528 | tf_op jit(solution)/shard_map/ppermute | solution.py:476
  15.0 12.3 %collective-permute-start.1 = (f32[4,160,128]{2,1,0:T(8,128)}, f32[4,160,128]{2,1,0:T(8,128)S(1)}, u32[]{:S(2)}, u32[]{:S(2)}) collective-permute-start(f32[4,160,128]{2,1,0:T(8,128)} %get-tuple-element.25), channel_id=1, source_target_pairs={{0,15},{1,0},{2,1},{3,2},{4,3},{5,4},{6,5},{7,6},{8,7},{9,8},{10,9... | collective-permute-start | bytes 983048 | tf_op jit(solution)/shard_map/ppermute | solution.py:476
  18.1 12.4 %all-to-all-start.1 = ((f32[8,64,256]{2,1,0:T(8,128)}), f32[8,64,256]{2,1,0:T(8,128)S(1)}, u32[]{:S(2)}, u32[]{:S(2)}) async-start(f32[8,64,256]{2,1,0:T(8,128)} %bitcast.6), calls=%async_computation.1 | async-start | bytes 1048576 | tf_op jit(solution)/shard_map/all_to_all | solution.py:524
  21.6 5.7 %copy-start.6 = (bf16[4,256,256]{2,1,0:T(8,128)(2,1)S(1)}, bf16[4,256,256]{2,1,0:T(8,128)(2,1)}, u32[]{:S(2)}) copy-start(bf16[4,256,256]{2,1,0:T(8,128)(2,1)} %constant.6.clone.zc) | copy-start | bytes 1572868
  27.3 28.1 %copy-start.7 = (bf16[4,256,256]{2,1,0:T(8,128)(2,1)S(1)}, bf16[4,256,256]{2,1,0:T(8,128)(2,1)}, u32[]{:S(2)}) copy-start(bf16[4,256,256]{2,1,0:T(8,128)(2,1)} %constant.7.clone.xc) | copy-start | bytes 1572868
  30.5 24.9 %copy-start.5 = (bf16[4,512,512]{2,1,0:T(8,128)(2,1)S(1)}, bf16[4,512,512]{2,1,0:T(8,128)(2,1)}, u32[]{:S(2)}) copy-start(bf16[4,512,512]{2,1,0:T(8,128)(2,1)} %constant.8.clone.yc) | copy-start | bytes 6291460
  60.6 23.6 %all-to-all-start.2 = ((f32[128,16,128]{2,1,0:T(8,128)}), f32[128,16,128]{2,1,0:T(8,128)S(1)}, u32[]{:S(2)}, u32[]{:S(2)}) async-start(f32[128,16,128]{2,1,0:T(8,128)} %bitcast.8), calls=%async_computation.2 | async-start | bytes 2097152 | tf_op jit(solution)/shard_map/all_to_all | solution.py:487
  84.2 2.7 %copy-start.8 = (bf16[2,256,2048]{2,1,0:T(8,128)(2,1)S(1)}, bf16[2,256,2048]{2,1,0:T(8,128)(2,1)}, u32[]{:S(2)}) copy-start(bf16[2,256,2048]{2,1,0:T(8,128)(2,1)} %get-tuple-element.20.wh_ref) | copy-start | bytes 6291460
  84.2 2.7 %copy-start.9 = (bf16[2,256,2048]{2,1,0:T(8,128)(2,1)S(1)}, bf16[2,256,2048]{2,1,0:T(8,128)(2,1)}, u32[]{:S(2)}) copy-start(bf16[2,256,2048]{2,1,0:T(8,128)(2,1)} %get-tuple-element.21.wl_ref) | copy-start | bytes 6291460
  84.2 2.9 %copy-start.10 = (bf16[2,256,2048]{2,1,0:T(8,128)(2,1)S(1)}, bf16[2,256,2048]{2,1,0:T(8,128)(2,1)}, u32[]{:S(2)}) copy-start(bf16[2,256,2048]{2,1,0:T(8,128)(2,1)} %get-tuple-element.22.sh_ref) | copy-start | bytes 6291460
  84.2 3.5 %copy-start.11 = (bf16[2,256,2048]{2,1,0:T(8,128)(2,1)S(1)}, bf16[2,256,2048]{2,1,0:T(8,128)(2,1)}, u32[]{:S(2)}) copy-start(bf16[2,256,2048]{2,1,0:T(8,128)(2,1)} %get-tuple-element.23.sl_ref) | copy-start | bytes 6291460
  84.2 4.1 %copy-start.12 = (f32[2,128,2048]{2,1,0:T(8,128)S(1)}, f32[2,128,2048]{2,1,0:T(8,128)}, u32[]{:S(2)}) copy-start(f32[2,128,2048]{2,1,0:T(8,128)} %get-tuple-element.19.xy_ref) | copy-start | bytes 6291460
  85.5 10.4 %collective-permute-start.5 = (f32[4,40,128]{2,1,0:T(8,128)S(1)}, f32[4,40,128]{2,1,0:T(8,128)S(1)}, u32[]{:S(2)}, u32[]{:S(2)}) collective-permute-start(f32[4,40,128]{2,1,0:T(8,128)S(1)} %get-tuple-element.30), channel_id=1, source_target_pairs={{0,17},{1,18},{2,19},{3,20},{4,21},{5,22},{6,23},{7,24},{8,25},{9,... | collective-permute-start | bytes 245768 | tf_op jit(solution)/shard_map/ppermute | solution.py:476
  85.8 10.2 %collective-permute-start.3 = (f32[4,80,128]{2,1,0:T(8,128)S(1)}, f32[4,80,128]{2,1,0:T(8,128)S(1)}, u32[]{:S(2)}, u32[]{:S(2)}) collective-permute-start(f32[4,80,128]{2,1,0:T(8,128)S(1)} %get-tuple-element.28), channel_id=1, source_target_pairs={{0,16},{1,17},{2,18},{3,19},{4,20},{5,21},{6,22},{7,23},{8,24},{9,... | collective-permute-start | bytes 491528 | tf_op jit(solution)/shard_map/ppermute | solution.py:476
  86.6 12.1 %collective-permute-start.4 = (f32[4,160,128]{2,1,0:T(8,128)S(1)}, f32[4,160,128]{2,1,0:T(8,128)S(1)}, u32[]{:S(2)}, u32[]{:S(2)}) collective-permute-start(f32[4,160,128]{2,1,0:T(8,128)S(1)} %get-tuple-element.29), channel_id=1, source_target_pairs={{0,1},{1,2},{2,3},{3,4},{4,5},{5,6},{6,7},{7,8},{8,9},{9,10},{10,1... | collective-permute-start | bytes 983048 | tf_op jit(solution)/shard_map/ppermute | solution.py:476
